TPU v7x, 32 devices: a whole 2x2x4 slice. The times are simulated.
32 devices in a mesh: depth: 4 (over y, x), screen: 8 (over z, core).
Axes of the slice: x: 2, y: 2, z: 4, core: 2. Of those that a mesh axis runs over, the one named last changes fastest.
Arguments:
- voxel_bins: int32 [32, 256, 2048], P('depth', None, 'screen'), may hold values from 0 to 255
- colors: bfloat16 [3, 256], replicated, may hold values from 0 to 2
- opacity: bfloat16 [256], replicated, may hold values from 0 to 1
- slab_order: int32 [8, 4], replicated, may hold values from 0 to 3, each once within a row
Outputs:
- image: float32 [4, 256, 2048], P(None, ('depth', 'screen'))
Inputs may be any that keep to these rules, and one draw needn't show every extreme that they name: `slab_order`: every row is a permutation of 0 to 3.
All inputs are finite; a program needn't handle non-finite values.
Results may differ from a plain program's by a relative error of at most 0.0003.
Values sent between devices are 32-bit elements; how exact they have to be, the bound alone decides.
No kernel may reach another device: no remote copies, remote signals or barrier semaphores. Data moves between devices by JAX's collectives and lax.ppermute only.
A program may use at most 64 MiB of HBM per device.

v0:
```python
import math

import jax
import jax.numpy as jnp
from jax import lax
from jax.sharding import PartitionSpec as P

low_count = 16
extinction = 3.0


def look_up(table_rows, bin_block):
    high_count = table_rows.shape[0] // 4
    low_part = bin_block % low_count
    high_part = bin_block // low_count
    low_onehot = (low_part[None, :] == jnp.arange(low_count, dtype=jnp.int32)[:, None]).astype(
        jnp.bfloat16
    )
    picked = jnp.dot(table_rows, low_onehot, preferred_element_type=jnp.float32)
    picked = picked.reshape(4, high_count, bin_block.shape[0])
    high_match = high_part[None, :] == jnp.arange(high_count, dtype=jnp.int32)[:, None]
    return jnp.sum(jnp.where(high_match[None], picked, 0.0), axis=1)


def render(voxel_bins, table_rows, total_samples):
    samples_here, row_count, col_count = voxel_bins.shape
    pixels = row_count * col_count
    per_step = math.gcd(samples_here, max(1, 131072 // pixels))
    blocks = voxel_bins.reshape(samples_here // per_step, per_step * pixels)
    extinct_rate = extinction / total_samples

    def advance(carried, bin_block):
        passed, color_sum = carried
        values = look_up(table_rows, bin_block).reshape(4, per_step, pixels)
        density = values[3]
        before = jnp.cumsum(density, axis=0) - density
        weight = (1.0 - jnp.exp(-extinct_rate * density)) * jnp.exp(
            -extinct_rate * (passed[None] + before)
        )
        color_sum = color_sum + jnp.sum(weight[None] * values[:3], axis=1)
        return ((passed + jnp.sum(density, axis=0), color_sum), None)

    start = (jnp.zeros((pixels,), jnp.float32), jnp.zeros((3, pixels), jnp.float32))
    (passed, color_sum), ignored = lax.scan(advance, start, blocks)
    final_alpha = 1.0 - jnp.exp(-extinct_rate * passed)
    partial_value = jnp.concatenate([color_sum, final_alpha[None]], axis=0)
    return partial_value.reshape(4, row_count, col_count)


def composite(pieces, places):
    in_front = (places[:, None, :] < places[:, :, None]).astype(jnp.float32)
    clear_log = jnp.log1p(-pieces[:, :, 3])
    front_log = jnp.einsum("tij,jtrw->itrw", in_front, clear_log, precision=lax.Precision.HIGHEST)
    shaded = jnp.sum(pieces[:, :, :3] * jnp.exp(front_log)[:, :, None], axis=0)
    total_alpha = 1.0 - jnp.exp(jnp.sum(clear_log, axis=0))
    merged = jnp.concatenate([shaded, total_alpha[:, None]], axis=1)
    return jnp.transpose(merged, (1, 2, 0, 3))


def local(voxel_bins, colors, opacity, slab_order):
    table = jnp.concatenate([colors, opacity[None]], axis=0)
    table_rows = table.reshape(4 * (table.shape[1] // low_count), low_count)
    depth_count = lax.axis_size("depth")
    total_samples = voxel_bins.shape[0] * depth_count
    partial_value = render(voxel_bins, table_rows, total_samples)
    own_order = lax.dynamic_slice_in_dim(slab_order, lax.axis_index("screen"), 1, 0)
    tile_block = composite(
        lax.all_to_all(partial_value[None], "depth", split_axis=2, concat_axis=0, tiled=True)[
            :, None
        ],
        own_order,
    )[:, :, 0]
    result = lax.all_to_all(tile_block, "screen", split_axis=1, concat_axis=2, tiled=True)
    return result


def solution(mesh):
    placed = (P("depth", None, "screen"), P(), P(), P())
    return jax.shard_map(
        local,
        mesh=mesh,
        in_specs=placed,
        out_specs=P(None, ("depth", "screen"), None),
        check_vma=False,
    )
```

profile of v0, /device:TPU:0, one launch (start us, length us, event | category | flops | bytes accessed | tf_op | source)
XLA Modules:
  0.0 185.4 jit_solution(1392531687887182417)
XLA Ops:
  0.0 4.0 %reshape.163 = s32[4,131072]{1,0:T(4,128)} reshape(s32[8,256,256]{2,1,0:T(8,128)} %param.6) | data formatting | bytes 4194304 | tf_op jit(solution)/shard_map/reshape | solution.py:29
  4.2 141.1 %while.15 = (s32[]{:T(128)}, f32[65536]{0:T(1024)}, f32[3,65536]{1,0:T(4,128)}, s32[4,131072]{1,0:T(4,128)}, bf16[64,16]{0,1:T(8,128)(2,1)S(1)}, /*index=5*/s32[]{:T(128)}, f32[]{:T(128)}, s32[]{:T(128)}) while((s32[]{:T(128)}, f32[65536]{0:T(1024)}, f32[3,65536]{1,0:T(4,128)}, s32[4,131072]{1,0:T(4,128)}, ...), condition=%wide.region_5.6_spmd.clone, body=%wide.region_0.5_spmd.clone.sunk | while | flops 293994496 | bytes 31983784 | solution.py:44
  4.2 3.4 %and_select_fusion.4 = (s32[1,131072]{1,0:T(1,128)S(1)}, s32[1,131072]{1,0:T(1,128)S(1)}) fusion(s32[4,131072]{1,0:T(4,128)} %get-tuple-element.186, s32[]{:T(128)} %get-tuple-element.175), kind=kLoop, calls=%fused_computation.5.clone.1 | loop fusion | flops 1441792 | bytes 1572868 | tf_op jit(solution)/shard_map/while/body/eval_jaxpr/jit(remainder)/select_n | solution.py:14
  7.6 3.8 %and_select_fusion.5 = s32[1,131072]{1,0:T(1,128)S(1)} fusion(s32[1,131072]{1,0:T(1,128)S(1)} %get-tuple-element.163, s32[4,131072]{1,0:T(4,128)} %get-tuple-element.186, s32[]{:T(128)} %get-tuple-element.175), kind=kLoop, calls=%fused_computation.6.clone.1 | loop fusion | flops 1572864 | bytes 1572868 | tf_op jit(solution)/shard_map/while/body/eval_jaxpr/jit(floor_divide)/jit(_where)/select_n | solution.py:15
  11.4 1.1 iota_compare_fusion.4
  12.5 11.0 %select_reduce_fusion.2 = f32[4,131072]{1,0:T(4,128)S(1)} fusion(pred[16,131072]{1,0:T(8,128)(4,1)S(1)} %iota_compare_fusion.4, bf16[64,16]{0,1:T(8,128)(2,1)S(1)} %get-tuple-element.187, s32[131072]{0:T(1024)S(1)} %bitcast.47), kind=kOutput, calls=%fused_computation.clone.1 | convolution fusion | flops 286785536 | bytes 4720640 | tf_op jit(solution)/shard_map/while/body/eval_jaxpr/dot_general | solution.py:19
  23.5 1.6 slice_reduce_fusion.2
  26.8 1.8 reduce_window_sum.13
  28.7 1.8 exponential_multiply_fusion.2
  30.5 2.9 %slice.46 = f32[3,2,65536]{2,1,0:T(2,128)} reshape(f32[3,131072]{1,0:T(4,128)S(1)} %bitcast.45) | data formatting | bytes 3145728 | tf_op jit(solution)/shard_map/while/body/eval_jaxpr/slice | solution.py:40
  33.3 3.9 %multiply_reduce_fusion.2 = f32[3,65536]{1,0:T(4,128)S(1)} fusion(f32[3,2,65536]{2,1,0:T(2,128)} %slice.46, f32[2,65536]{1,0:T(2,128)S(1)} %exponential_multiply_fusion.2), kind=kLoop, calls=%fused_computation.7.clone.1 | loop fusion | flops 589824 | bytes 2883584 | tf_op jit(solution)/shard_map/while/body/eval_jaxpr/reduce_sum | solution.py:40
  37.9 0.9 copy-done.2
  38.8 3.4 %and_select_fusion.4 = (s32[1,131072]{1,0:T(1,128)S(1)}, s32[1,131072]{1,0:T(1,128)S(1)}) fusion(s32[4,131072]{1,0:T(4,128)} %get-tuple-element.186, s32[]{:T(128)} %get-tuple-element.175), kind=kLoop, calls=%fused_computation.5.clone.1 | loop fusion | flops 1441792 | bytes 1572868 | tf_op jit(solution)/shard_map/while/body/eval_jaxpr/jit(remainder)/select_n | solution.py:14
  42.2 3.8 %and_select_fusion.5 = s32[1,131072]{1,0:T(1,128)S(1)} fusion(s32[1,131072]{1,0:T(1,128)S(1)} %get-tuple-element.163, s32[4,131072]{1,0:T(4,128)} %get-tuple-element.186, s32[]{:T(128)} %get-tuple-element.175), kind=kLoop, calls=%fused_computation.6.clone.1 | loop fusion | flops 1572864 | bytes 1572868 | tf_op jit(solution)/shard_map/while/body/eval_jaxpr/jit(floor_divide)/jit(_where)/select_n | solution.py:15
  45.9 1.1 iota_compare_fusion.4
  47.0 11.0 %select_reduce_fusion.2 = f32[4,131072]{1,0:T(4,128)S(1)} fusion(pred[16,131072]{1,0:T(8,128)(4,1)S(1)} %iota_compare_fusion.4, bf16[64,16]{0,1:T(8,128)(2,1)S(1)} %get-tuple-element.187, s32[131072]{0:T(1024)S(1)} %bitcast.47), kind=kOutput, calls=%fused_computation.clone.1 | convolution fusion | flops 286785536 | bytes 4720640 | tf_op jit(solution)/shard_map/while/body/eval_jaxpr/dot_general | solution.py:19
  58.1 1.6 slice_reduce_fusion.2
  60.6 1.7 fusion.17
  62.3 1.8 reduce_window_sum.13
  64.2 1.8 exponential_multiply_fusion.2
  66.0 2.9 %slice.46 = f32[3,2,65536]{2,1,0:T(2,128)} reshape(f32[3,131072]{1,0:T(4,128)S(1)} %bitcast.45) | data formatting | bytes 3145728 | tf_op jit(solution)/shard_map/while/body/eval_jaxpr/slice | solution.py:40
  68.8 3.9 %multiply_reduce_fusion.2 = f32[3,65536]{1,0:T(4,128)S(1)} fusion(f32[3,2,65536]{2,1,0:T(2,128)} %slice.46, f32[2,65536]{1,0:T(2,128)S(1)} %exponential_multiply_fusion.2), kind=kLoop, calls=%fused_computation.7.clone.1 | loop fusion | flops 589824 | bytes 2883584 | tf_op jit(solution)/shard_map/while/body/eval_jaxpr/reduce_sum | solution.py:40
  73.4 0.9 copy-done.2
  74.3 3.4 %and_select_fusion.4 = (s32[1,131072]{1,0:T(1,128)S(1)}, s32[1,131072]{1,0:T(1,128)S(1)}) fusion(s32[4,131072]{1,0:T(4,128)} %get-tuple-element.186, s32[]{:T(128)} %get-tuple-element.175), kind=kLoop, calls=%fused_computation.5.clone.1 | loop fusion | flops 1441792 | bytes 1572868 | tf_op jit(solution)/shard_map/while/body/eval_jaxpr/jit(remainder)/select_n | solution.py:14
  77.7 3.8 %and_select_fusion.5 = s32[1,131072]{1,0:T(1,128)S(1)} fusion(s32[1,131072]{1,0:T(1,128)S(1)} %get-tuple-element.163, s32[4,131072]{1,0:T(4,128)} %get-tuple-element.186, s32[]{:T(128)} %get-tuple-element.175), kind=kLoop, calls=%fused_computation.6.clone.1 | loop fusion | flops 1572864 | bytes 1572868 | tf_op jit(solution)/shard_map/while/body/eval_jaxpr/jit(floor_divide)/jit(_where)/select_n | solution.py:15
  81.4 1.1 iota_compare_fusion.4
  82.5 11.0 %select_reduce_fusion.2 = f32[4,131072]{1,0:T(4,128)S(1)} fusion(pred[16,131072]{1,0:T(8,128)(4,1)S(1)} %iota_compare_fusion.4, bf16[64,16]{0,1:T(8,128)(2,1)S(1)} %get-tuple-element.187, s32[131072]{0:T(1024)S(1)} %bitcast.47), kind=kOutput, calls=%fused_computation.clone.1 | convolution fusion | flops 286785536 | bytes 4720640 | tf_op jit(solution)/shard_map/while/body/eval_jaxpr/dot_general | solution.py:19
  93.6 1.6 slice_reduce_fusion.2
  96.1 1.7 fusion.17
  97.8 1.8 reduce_window_sum.13
  99.7 1.8 exponential_multiply_fusion.2
  101.5 2.9 %slice.46 = f32[3,2,65536]{2,1,0:T(2,128)} reshape(f32[3,131072]{1,0:T(4,128)S(1)} %bitcast.45) | data formatting | bytes 3145728 | tf_op jit(solution)/shard_map/while/body/eval_jaxpr/slice | solution.py:40
  104.3 3.9 %multiply_reduce_fusion.2 = f32[3,65536]{1,0:T(4,128)S(1)} fusion(f32[3,2,65536]{2,1,0:T(2,128)} %slice.46, f32[2,65536]{1,0:T(2,128)S(1)} %exponential_multiply_fusion.2), kind=kLoop, calls=%fused_computation.7.clone.1 | loop fusion | flops 589824 | bytes 2883584 | tf_op jit(solution)/shard_map/while/body/eval_jaxpr/reduce_sum | solution.py:40
  109.8 3.4 %and_select_fusion.4 = (s32[1,131072]{1,0:T(1,128)S(1)}, s32[1,131072]{1,0:T(1,128)S(1)}) fusion(s32[4,131072]{1,0:T(4,128)} %get-tuple-element.186, s32[]{:T(128)} %get-tuple-element.175), kind=kLoop, calls=%fused_computation.5.clone.1 | loop fusion | flops 1441792 | bytes 1572868 | tf_op jit(solution)/shard_map/while/body/eval_jaxpr/jit(remainder)/select_n | solution.py:14
  113.2 3.8 %and_select_fusion.5 = s32[1,131072]{1,0:T(1,128)S(1)} fusion(s32[1,131072]{1,0:T(1,128)S(1)} %get-tuple-element.163, s32[4,131072]{1,0:T(4,128)} %get-tuple-element.186, s32[]{:T(128)} %get-tuple-element.175), kind=kLoop, calls=%fused_computation.6.clone.1 | loop fusion | flops 1572864 | bytes 1572868 | tf_op jit(solution)/shard_map/while/body/eval_jaxpr/jit(floor_divide)/jit(_where)/select_n | solution.py:15
  116.9 1.1 iota_compare_fusion.4
  118.0 11.0 %select_reduce_fusion.2 = f32[4,131072]{1,0:T(4,128)S(1)} fusion(pred[16,131072]{1,0:T(8,128)(4,1)S(1)} %iota_compare_fusion.4, bf16[64,16]{0,1:T(8,128)(2,1)S(1)} %get-tuple-element.187, s32[131072]{0:T(1024)S(1)} %bitcast.47), kind=kOutput, calls=%fused_computation.clone.1 | convolution fusion | flops 286785536 | bytes 4720640 | tf_op jit(solution)/shard_map/while/body/eval_jaxpr/dot_general | solution.py:19
  129.1 1.6 slice_reduce_fusion.2
  131.6 1.7 fusion.17
  133.3 1.8 reduce_window_sum.13
  135.2 1.8 exponential_multiply_fusion.2
  137.0 2.9 %slice.46 = f32[3,2,65536]{2,1,0:T(2,128)} reshape(f32[3,131072]{1,0:T(4,128)S(1)} %bitcast.45) | data formatting | bytes 3145728 | tf_op jit(solution)/shard_map/while/body/eval_jaxpr/slice | solution.py:40
  139.8 3.9 %multiply_reduce_fusion.2 = f32[3,65536]{1,0:T(4,128)S(1)} fusion(f32[3,2,65536]{2,1,0:T(2,128)} %slice.46, f32[2,65536]{1,0:T(2,128)S(1)} %exponential_multiply_fusion.2), kind=kLoop, calls=%fused_computation.7.clone.1 | loop fusion | flops 589824 | bytes 2883584 | tf_op jit(solution)/shard_map/while/body/eval_jaxpr/reduce_sum | solution.py:40
  145.3 1.0 exponential_subtract_fusion
  146.3 2.7 %pad_maximum_fusion = f32[1,4,256,256]{3,1,0,2:T(4,128)} fusion(f32[1,1,256,256]{3,1,0,2:T(1,128)S(1)} %bitcast.53, f32[1,3,256,256]{3,1,0,2:T(4,128)} %bitcast.48), kind=kLoop, calls=%fused_computation.17 | loop fusion | flops 262144 | bytes 2097152 | tf_op jit(solution)/shard_map/concatenate | solution.py:46
  149.0 5.2 %all-to-all-start = ((f32[1,4,256,256]{3,1,0,2:T(4,128)}), f32[1,4,256,256]{3,1,0,2:T(4,128)S(1)}, u32[]{:S(2)}, u32[]{:S(2)}) async-start(f32[1,4,256,256]{3,1,0,2:T(4,128)} %pad_maximum_fusion), calls=%async_computation | async-start | bytes 2097152 | tf_op jit(solution)/shard_map/all_to_all | solution.py:68
  154.4 13.4 %all-to-all-done = f32[1,4,256,256]{3,1,0,2:T(4,128)S(1)} async-done(((f32[1,4,256,256]{3,1,0,2:T(4,128)}), f32[1,4,256,256]{3,1,0,2:T(4,128)S(1)}, u32[]{:S(2)}, u32[]{:S(2)}) %all-to-all-start) | async-done | bytes 1048608 | tf_op jit(solution)/shard_map/all_to_all | solution.py:68
  170.2 14.4 %all_to_all.33 = f32[4,64,256]{2,0,1:T(4,128)S(1)} all-to-all(f32[4,64,256]{2,0,1:T(4,128)S(1)} %copy.19), channel_id=1, replica_groups=mesh['depth'=4,'screen'=8] {'screen'}, dimensions={1} | all-to-all | bytes 524288 | tf_op jit(solution)/shard_map/all_to_all | solution.py:73
  (48 shorter events, 12.3 us)
Async XLA Ops:
  0.0 154.2 %copy-start = (s32[8,4]{0,1:T(4,128)S(1)}, s32[8,4]{0,1:T(4,128)}, u32[]{:S(2)}) copy-start(s32[8,4]{0,1:T(4,128)} %param.9) | copy-start | bytes 388
  0.0 4.0 %copy-start.4 = (bf16[256]{0:T(256)(128)(2,1)S(1)}, bf16[256]{0:T(256)(128)(2,1)}, u32[]{:S(2)}) copy-start(bf16[256]{0:T(256)(128)(2,1)} %param.8) | copy-start | bytes 1540
  0.0 4.0 %copy-start.3 = (bf16[3,256]{1,0:T(4,128)(2,1)S(1)}, bf16[3,256]{1,0:T(4,128)(2,1)}, u32[]{:S(2)}) copy-start(bf16[3,256]{1,0:T(4,128)(2,1)} %param.7) | copy-start | bytes 4612
  33.3 3.9 %copy-start.1 = (f32[3,65536]{1,0:T(4,128)S(1)}, f32[3,65536]{1,0:T(4,128)}, u32[]{:S(2)}) copy-start(f32[3,65536]{1,0:T(4,128)} %get-tuple-element.177) | copy-start | bytes 2359300 | tf_op jit(solution)/shard_map/while
  37.8 1.0 copy-start.2
  68.8 3.9 %copy-start.1 = (f32[3,65536]{1,0:T(4,128)S(1)}, f32[3,65536]{1,0:T(4,128)}, u32[]{:S(2)}) copy-start(f32[3,65536]{1,0:T(4,128)} %get-tuple-element.177) | copy-start | bytes 2359300 | tf_op jit(solution)/shard_map/while
  73.4 1.0 copy-start.2
  104.3 3.9 %copy-start.1 = (f32[3,65536]{1,0:T(4,128)S(1)}, f32[3,65536]{1,0:T(4,128)}, u32[]{:S(2)}) copy-start(f32[3,65536]{1,0:T(4,128)} %get-tuple-element.177) | copy-start | bytes 2359300 | tf_op jit(solution)/shard_map/while
  108.9 1.0 copy-start.2
  139.8 3.9 %copy-start.1 = (f32[3,65536]{1,0:T(4,128)S(1)}, f32[3,65536]{1,0:T(4,128)}, u32[]{:S(2)}) copy-start(f32[3,65536]{1,0:T(4,128)} %get-tuple-element.177) | copy-start | bytes 2359300 | tf_op jit(solution)/shard_map/while
  144.4 1.0 copy-start.2
  149.0 18.8 %all-to-all-start = ((f32[1,4,256,256]{3,1,0,2:T(4,128)}), f32[1,4,256,256]{3,1,0,2:T(4,128)S(1)}, u32[]{:S(2)}, u32[]{:S(2)}) async-start(f32[1,4,256,256]{3,1,0,2:T(4,128)} %pad_maximum_fusion), calls=%async_computation | async-start | bytes 2097152 | tf_op jit(solution)/shard_map/all_to_all | solution.py:68
where the time goes:
time: 186 us; the launch traced here: 185 us
  other arithmetic  78.4 us (42%)
  matrix products  44.8 us (24%)
  local copies, waits for them, and re-layouts  28.7 us (15%)
  blocking collectives  14.4 us (8%)
  waiting for transfers between devices  13.4 us (7%)
  starting transfers between devices  5.19 us (3%)
    dot_general x4, matrix products, look_up(): picked = jnp.dot(table_rows, low_onehot, preferred_element_type=jnp.float32)  44.2 us
    reduce_sum x4, other arithmetic, advance(): color_sum = color_sum + jnp.sum(weight[None] * values[:3], axis=1)  15.5 us
    select_n x4, other arithmetic, look_up(): high_part = bin_block // low_count  15 us
    all_to_all x1, blocking collectives, local(): lax.all_to_all(tile_block, 'screen', split_axis=1, concat_axis=2, tiled=T...  14.4 us
    select_n x4, other arithmetic, look_up(): low_part = bin_block % low_count  13.5 us
    all_to_all x1, waiting for transfers between devices, local(): lax.all_to_all(partial_value[None], 'depth', split_axis=2, concat_axis=0,...  13.4 us
    slice x4, local copies, waits for them, and re-layouts, advance(): color_sum = color_sum + jnp.sum(weight[None] * values[:3], axis=1)  11.4 us
    another operation x4, other arithmetic, advance(): before = jnp.cumsum(density, axis=0) - density  7.29 us
  transfers between devices with their start and end apart: 1, of which 1 were waited for; matrix products, arithmetic and copies ran while one was open for 0% of the time, Pallas kernels for 0%

commit v1 on v0

v1 whole, which is shorter than its diff:
```python
import functools

import jax
import jax.numpy as jnp
from jax import lax
from jax.experimental import pallas as pl
from jax.experimental.pallas import tpu as pltpu
from jax.sharding import PartitionSpec as P

extinction = 3.0
lanes = 128
sublanes = 8


def partner_of(index, step, count):
    if count & (count - 1) == 0:
        return index ^ step
    return (index + step) % count


def source_of(index, step, count):
    if count & (count - 1) == 0:
        return index ^ step
    return (index - step) % count


def render_kernel(block_ref, colors_ref, opacity_ref, bins_ref, out_ref, *, rate):
    samples_here, row_count, col_count = bins_ref.shape
    clear = jnp.exp(-rate * opacity_ref[...].astype(jnp.float32))
    shade = (1.0 - clear) * colors_ref[...].astype(jnp.float32)
    full = jnp.concatenate([shade, clear], axis=0)
    bin_count = full.shape[1]
    halves = bin_count // lanes
    tables = [
        [
            jnp.broadcast_to(full[c : c + 1, h * lanes : (h + 1) * lanes], (sublanes, lanes))
            for h in range(halves)
        ]
        for c in range(4)
    ]

    def advance(group, ignored):
        rows = pl.ds(pl.multiple_of(group * sublanes, sublanes), sublanes)
        for col in range(0, col_count, lanes):
            cols = slice(col, col + lanes)
            for sample in range(samples_here):
                index = bins_ref[sample, rows, cols]
                low = index & (lanes - 1)
                high = index // lanes if halves > 2 else index >= lanes
                picked = []
                for c in range(4):
                    value = jnp.take_along_axis(tables[c][0], low, axis=1, mode="promise_in_bounds")
                    for h in range(1, halves):
                        other = jnp.take_along_axis(
                            tables[c][h], low, axis=1, mode="promise_in_bounds"
                        )
                        value = jnp.where(high if halves == 2 else high == h, other, value)
                    picked.append(value)
                if sample == 0:
                    sums = picked[:3]
                    through = picked[3]
                else:
                    sums = [s + through * v for s, v in zip(sums, picked[:3])]
                    through = through * picked[3]
            for c in range(3):
                out_ref[c, rows, cols] = sums[c]
            out_ref[3, rows, cols] = 1.0 - through
        return ignored

    lax.fori_loop(0, row_count // sublanes, advance, 0)


def render_block(voxel_bins, colors, opacity_row, block, block_rows, rate):
    samples_here, row_count, col_count = voxel_bins.shape
    steps = 2 if block_rows % (2 * sublanes) == 0 else 1
    step_rows = block_rows // steps
    return pl.pallas_call(
        functools.partial(render_kernel, rate=rate),
        out_shape=pltpu.VMEM((4, block_rows, col_count), jnp.float32),
        grid_spec=pltpu.PrefetchScalarGridSpec(
            num_scalar_prefetch=1,
            grid=(steps,),
            in_specs=[
                pl.BlockSpec(colors.shape, lambda i, b: (0, 0)),
                pl.BlockSpec(opacity_row.shape, lambda i, b: (0, 0)),
                pl.BlockSpec(
                    (samples_here, step_rows, col_count), lambda i, b: (0, b[0] * steps + i, 0)
                ),
            ],
            out_specs=pl.BlockSpec((4, step_rows, col_count), lambda i, b: (0, i, 0)),
        ),
        compiler_params=pltpu.CompilerParams(dimension_semantics=("arbitrary",)),
        name="render_block",
    )(block, colors, opacity_row, voxel_bins)


def composite_kernel(places_ref, *refs):
    pieces, out_ref = refs[:-1], refs[-1]
    count = len(pieces)
    target_count, ignored, owned_rows, col_count = out_ref.shape
    together = max(1, sublanes // owned_rows)
    group_rows = together * owned_rows

    def advance(group, ignored):
        rows = pl.ds(pl.multiple_of(group * group_rows, group_rows), group_rows)

        def put(channel, value):
            for i in range(together):
                out_ref[group * together + i, channel] = value[
                    i * owned_rows : (i + 1) * owned_rows
                ]

        clear = [1.0 - piece[3, rows, :] for piece in pieces]
        before = [None] * count
        for j in range(count):
            for k in range(j + 1, count):
                first = places_ref[j] < places_ref[k]
                onto_k = jnp.where(first, clear[j], 1.0)
                onto_j = jnp.where(first, 1.0, clear[k])
                before[k] = onto_k if before[k] is None else before[k] * onto_k
                before[j] = onto_j if before[j] is None else before[j] * onto_j
        for c in range(3):
            total = before[0] * pieces[0][c, rows, :]
            for j in range(1, count):
                total = total + before[j] * pieces[j][c, rows, :]
            put(c, total)
        through = clear[0]
        for j in range(1, count):
            through = through * clear[j]
        put(3, 1.0 - through)
        return ignored

    lax.fori_loop(0, target_count // together, advance, 0)


def composite(pieces, places, target_count):
    channels, block_rows, col_count = pieces[0].shape
    return pl.pallas_call(
        composite_kernel,
        out_shape=pltpu.VMEM(
            (target_count, 4, block_rows // target_count, col_count), jnp.float32
        ),
        in_specs=[pl.BlockSpec(memory_space=pltpu.SMEM)]
        + [pl.BlockSpec(memory_space=pltpu.VMEM)] * len(pieces),
        out_specs=pl.BlockSpec(memory_space=pltpu.VMEM),
        name="composite",
    )(places, *[pltpu.with_memory_space_constraint(p, pltpu.VMEM) for p in pieces])


def assemble_kernel(tiles_ref, *refs):
    parts, out_ref = refs[:-1], refs[-1]
    col_count = parts[0].shape[-1]
    for i, part in enumerate(parts):
        cols = pl.ds(pl.multiple_of(tiles_ref[i] * col_count, col_count), col_count)
        out_ref[:, :, cols] = part[...]


def assemble(parts, tiles):
    channels, owned_rows, col_count = parts[0].shape
    return pl.pallas_call(
        assemble_kernel,
        out_shape=jax.ShapeDtypeStruct(
            (channels, owned_rows, col_count * len(parts)), jnp.float32
        ),
        in_specs=[pl.BlockSpec(memory_space=pltpu.SMEM)]
        + [pl.BlockSpec(memory_space=pltpu.VMEM)] * len(parts),
        out_specs=pl.BlockSpec(memory_space=pltpu.VMEM),
        name="assemble",
    )(tiles, *[pltpu.with_memory_space_constraint(p, pltpu.VMEM) for p in parts])


def local(voxel_bins, colors, opacity, slab_order):
    depth_count = lax.axis_size("depth")
    screen_count = lax.axis_size("screen")
    samples_here, row_count, col_count = voxel_bins.shape
    rate = extinction / (samples_here * depth_count)
    depth_index = lax.axis_index("depth")
    screen_index = lax.axis_index("screen")
    block_rows = row_count // depth_count
    opacity_row = opacity[None]

    pieces = [None] * depth_count
    for step in list(range(depth_count - 1, 0, -1)) + [0]:
        block = partner_of(depth_index, step, depth_count).astype(jnp.int32)[None]
        piece = render_block(voxel_bins, colors, opacity_row, block, block_rows, rate)
        if step:
            pairs = [(i, partner_of(i, step, depth_count)) for i in range(depth_count)]
            piece = lax.ppermute(piece, "depth", pairs)
        pieces[step] = piece
    own_order = lax.dynamic_index_in_dim(slab_order, screen_index, 0, keepdims=False)
    sources = jnp.stack([source_of(depth_index, step, depth_count) for step in range(depth_count)])
    places = own_order[sources]
    blocks = composite(pieces, places, screen_count)
    parts = [lax.dynamic_index_in_dim(blocks, screen_index, 0, keepdims=False)]
    for step in range(1, screen_count):
        target = partner_of(screen_index, step, screen_count)
        pairs = [(i, partner_of(i, step, screen_count)) for i in range(screen_count)]
        part = lax.dynamic_index_in_dim(blocks, target, 0, keepdims=False)
        parts.append(lax.ppermute(part, "screen", pairs))
    tiles = jnp.stack([source_of(screen_index, step, screen_count) for step in range(screen_count)])
    return assemble(parts, tiles)


def solution(mesh):
    placed = (P("depth", None, "screen"), P(), P(), P())
    return jax.shard_map(
        local,
        mesh=mesh,
        in_specs=placed,
        out_specs=P(None, ("depth", "screen"), None),
        check_vma=False,
    )
```

time: 186 us -> 39.7 us (0.21)
  other arithmetic: 78.4 us -> 0.09 us
  matrix products: 44.8 us -> 0 us
  local copies, waits for them, and re-layouts: 28.7 us -> 3.18 us
  Pallas kernels: 0 us -> 14.6 us
  blocking collectives: 14.4 us -> 0 us
  starting transfers between devices: 5.19 us -> 12.9 us
  waiting for transfers between devices: 13.4 us -> 8.59 us
    dot_general x5 -> x0, matrix products: 44.8 us -> none  [the longest x4 44.2 us: look_up(): picked = jnp.dot(table_rows, low_onehot, preferred_element_type=jnp.float32)]
    select_n x8 -> x1, other arithmetic: 28.5 us -> 0.08 us  [local(): places = own_order[sources]]
    reduce_sum x10 -> x0, other arithmetic: 18.9 us -> none  [the longest x4 15.5 us: advance(): color_sum = color_sum + jnp.sum(weight[None] * values[:3], axis=1)]
    slice x8 -> x0, local copies, waits for them, and re-layouts: 17.7 us -> none  [the longest x4 11.4 us: advance(): color_sum = color_sum + jnp.sum(weight[None] * values[:3], axis=1)]
    pallas_call x0 -> x6, Pallas kernels: none -> 14.6 us  [the longest x4 12.4 us: render_block(): pl.pallas_call(functools.partial(render_kernel, rate=rate), out_shape=plt...]
    all_to_all x1 -> x0, blocking collectives: 14.4 us -> none  [local(): lax.all_to_all(tile_block, 'screen', split_axis=1, concat_axis=2, tiled=T...]
    all_to_all x1 -> x0, waiting for transfers between devices: 13.4 us -> none  [local(): lax.all_to_all(partial_value[None], 'depth', split_axis=2, concat_axis=0,...]
    ppermute x0 -> x10, starting transfers between devices: none -> 12.9 us  [the longest x7 8.24 us: local(): parts.append(lax.ppermute(part, 'screen', pairs))]
  transfers between devices with their start and end apart: 1 -> 10, of which waited for: 1 -> 3; matrix products, arithmetic and copies ran while one was open for 0% -> 5% of each run, Pallas kernels for 0% -> 24%
where the time goes in v1:
time: 39.7 us; the launch traced here: 39.5 us
  Pallas kernels  14.6 us (37%)
  starting transfers between devices  12.9 us (32%)
  waiting for transfers between devices  8.59 us (22%)
  local copies, waits for them, and re-layouts  3.18 us (8%)
    pallas_call x4, Pallas kernels, render_block(): pl.pallas_call(functools.partial(render_kernel, rate=rate), out_shape=plt...  12.4 us
    ppermute x7, starting transfers between devices, local(): parts.append(lax.ppermute(part, 'screen', pairs))  8.24 us
    ppermute x3, starting transfers between devices, local(): piece = lax.ppermute(piece, 'depth', pairs)  4.69 us
    ppermute x7, waiting for transfers between devices, local(): parts.append(lax.ppermute(part, 'screen', pairs))  4.48 us
    ppermute x3, waiting for transfers between devices, local(): piece = lax.ppermute(piece, 'depth', pairs)  4.11 us
    pallas_call x1, Pallas kernels, assemble(): pl.pallas_call(assemble_kernel, out_shape=jax.ShapeDtypeStruct((channels,...  1.39 us
    broadcast_in_dim x1, local copies, waits for them, and re-layouts, local(): opacity_row = opacity[None]  1.23 us
    gather x1, local copies, waits for them, and re-layouts, local(): places = own_order[sources]  1.15 us
  transfers between devices with their start and end apart: 10, of which 3 were waited for; matrix products, arithmetic and copies ran while one was open for 5% of the time, Pallas kernels for 24%

profile of v1, /device:TPU:0, one launch (start us, length us, event | category | flops | bytes accessed | tf_op | source)
XLA Modules:
  0.0 39.5 jit_solution(15729255698067353)
XLA Ops:
  0.0 0.0 copy-start
  0.0 1.2 %broadcast_in_dim.2.opacity_ref = bf16[1,256]{1,0:T(2,128)(2,1)} reshape(bf16[256]{0:T(256)(128)(2,1)} %param.6) | data formatting | bytes 1024 | tf_op jit(solution)/shard_map/broadcast_in_dim | solution.py:180
  1.2 3.1 %render_block.5 = f32[4,64,256]{2,1,0:T(8,128)S(1)} custom-call(s32[1]{0:T(128)} %bitcast.14.block_ref, bf16[3,256]{1,0:T(4,128)(2,1)} %colors_ref.7, bf16[1,256]{1,0:T(2,128)(2,1)} %broadcast_in_dim.2.opacity_ref, s32[8,256,256]{2,1,0:T(8,128)} %bins_ref.7), custom_call_target="tpu_custom_call" | custom-call | tf_op jit(solution)/shard_map/render_block/pallas_call | solution.py:77
  4.3 3.0 %collective-permute-start = (f32[4,64,256]{2,1,0:T(8,128)S(1)}, f32[4,64,256]{2,1,0:T(8,128)S(1)}, u32[]{:S(2)}, u32[]{:S(2)}) collective-permute-start(f32[4,64,256]{2,1,0:T(8,128)S(1)} %render_block.5), channel_id=1, source_target_pairs={{0,8},{8,0},{16,24},{24,16},{1,9},{9,1},{17,25},{25,17},{2,10},{10... | collective-permute-start | bytes 786440 | tf_op jit(solution)/shard_map/ppermute | solution.py:188
  7.4 3.1 %render_block.6 = f32[4,64,256]{2,1,0:T(8,128)S(1)} custom-call(s32[1]{0:T(128)} %bitcast.15.block_ref, bf16[3,256]{1,0:T(4,128)(2,1)} %colors_ref.7, bf16[1,256]{1,0:T(2,128)(2,1)} %broadcast_in_dim.2.opacity_ref, s32[8,256,256]{2,1,0:T(8,128)} %bins_ref.7), custom_call_target="tpu_custom_call" | custom-call | tf_op jit(solution)/shard_map/render_block/pallas_call | solution.py:77
  10.5 1.6 %collective-permute-start.1 = (f32[4,64,256]{2,1,0:T(8,128)S(1)}, f32[4,64,256]{2,1,0:T(8,128)S(1)}, u32[]{:S(2)}, u32[]{:S(2)}) collective-permute-start(f32[4,64,256]{2,1,0:T(8,128)S(1)} %render_block.6), channel_id=1, source_target_pairs={{0,16},{8,24},{16,0},{24,8},{1,17},{9,25},{17,1},{25,9},{2,18},{10... | collective-permute-start | bytes 786440 | tf_op jit(solution)/shard_map/ppermute | solution.py:188
  12.0 3.1 %render_block.7 = f32[4,64,256]{2,1,0:T(8,128)S(1)} custom-call(s32[1]{0:T(128)} %bitcast.16.block_ref, bf16[3,256]{1,0:T(4,128)(2,1)} %colors_ref.7, bf16[1,256]{1,0:T(2,128)(2,1)} %broadcast_in_dim.2.opacity_ref, s32[8,256,256]{2,1,0:T(8,128)} %bins_ref.7), custom_call_target="tpu_custom_call" | custom-call | tf_op jit(solution)/shard_map/render_block/pallas_call | solution.py:77
  15.1 0.1 collective-permute-start.2
  15.2 3.1 %render_block.4.refs_0_ = f32[4,64,256]{2,1,0:T(8,128)S(1)} custom-call(s32[1]{0:T(128)} %bitcast.13.block_ref, bf16[3,256]{1,0:T(4,128)(2,1)} %colors_ref.7, bf16[1,256]{1,0:T(2,128)(2,1)} %broadcast_in_dim.2.opacity_ref, s32[8,256,256]{2,1,0:T(8,128)} %bins_ref.7), custom_call_target="tpu_custom_call" | custom-call | tf_op jit(solution)/shard_map/render_block/pallas_call | solution.py:77
  18.4 0.0 copy-done
  18.4 0.2 fusion
  18.6 0.1 fusion.1
  18.6 1.1 %gather_fusion = s32[4]{0:T(128)} fusion(s32[4]{0:T(128)S(1)} %fusion, s32[1024]{0:T(1024)S(1)} %pad_clamp_fusion), kind=kCustom, calls=%fused_computation | custom fusion | bytes 48 | tf_op jit(solution)/shard_map/gather | solution.py:192
  19.8 0.0 collective-permute-done.refs_1_
  19.8 4.1 %collective-permute-done.1.refs_2_ = f32[4,64,256]{2,1,0:T(8,128)S(1)} collective-permute-done((f32[4,64,256]{2,1,0:T(8,128)S(1)}, f32[4,64,256]{2,1,0:T(8,128)S(1)}, u32[]{:S(2)}, u32[]{:S(2)}) %collective-permute-start.1) | collective-permute-done | bytes 262176 | tf_op jit(solution)/shard_map/ppermute | solution.py:188
  23.9 0.0 collective-permute-done.2.refs_3_
  23.9 0.8 %composite.1 = f32[8,4,8,256]{3,2,1,0:T(8,128)S(1)} custom-call(s32[4]{0:T(128)} %gather_fusion, f32[4,64,256]{2,1,0:T(8,128)S(1)} %render_block.4.refs_0_, f32[4,64,256]{2,1,0:T(8,128)S(1)} %collective-permute-done.refs_1_, f32[4,64,256]{2,1,0:T(8,128)S(1)} %collective-permute-done.1.refs_2_, f32[4,64,256]{2,1,0:T(8,128)S(1)} %collective-permute-done.2.refs_3_), custom_call_target="tpu_custom_call" | custom-call | tf_op jit(solution)/shard_map/composite/pallas_call | solution.py:138
  24.8 0.1 collective-permute-start.3
  24.9 1.6 %collective-permute-start.4 = (f32[4,8,256]{2,1,0:T(8,128)S(1)}, f32[4,8,256]{2,1,0:T(8,128)S(1)}, u32[]{:S(2)}, u32[]{:S(2)}) collective-permute-start(f32[4,8,256]{2,1,0:T(8,128)S(1)} %get-tuple-element.10), channel_id=1, source_target_pairs={{0,2},{1,3},{2,0},{3,1},{4,6},{5,7},{6,4},{7,5},{8,10},{9,11},{10,... | collective-permute-start | bytes 98312 | tf_op jit(solution)/shard_map/ppermute | solution.py:199
  26.5 0.2 collective-permute-start.5
  26.7 2.6 %collective-permute-start.6 = (f32[4,8,256]{2,1,0:T(8,128)S(1)}, f32[4,8,256]{2,1,0:T(8,128)S(1)}, u32[]{:S(2)}, u32[]{:S(2)}) collective-permute-start(f32[4,8,256]{2,1,0:T(8,128)S(1)} %get-tuple-element.8), channel_id=1, source_target_pairs={{0,4},{1,5},{2,6},{3,7},{4,0},{5,1},{6,2},{7,3},{8,12},{9,13},{10,... | collective-permute-start | bytes 98312 | tf_op jit(solution)/shard_map/ppermute | solution.py:199
  29.3 0.0 collective-permute-start.7
  29.3 0.0 collective-permute-done.3.refs_1_
  29.3 3.6 %collective-permute-start.8 = (f32[4,8,256]{2,1,0:T(8,128)S(1)}, f32[4,8,256]{2,1,0:T(8,128)S(1)}, u32[]{:S(2)}, u32[]{:S(2)}) collective-permute-start(f32[4,8,256]{2,1,0:T(8,128)S(1)} %get-tuple-element.6), channel_id=1, source_target_pairs={{0,6},{1,7},{2,4},{3,5},{4,2},{5,3},{6,0},{7,1},{8,14},{9,15},{10,... | collective-permute-start | bytes 98312 | tf_op jit(solution)/shard_map/ppermute | solution.py:199
  32.9 0.0 collective-permute-done.4.refs_2_
  32.9 0.1 collective-permute-start.9
  33.0 0.6 %stack.58.tiles_ref = s32[8]{0:T(128)} concatenate(s32[1]{0:T(128)} %bitcast, s32[1]{0:T(128)} %bitcast.1, s32[1]{0:T(128)} %bitcast.2, s32[1]{0:T(128)} %bitcast.3, s32[1]{0:T(128)} %bitcast.4, s32[1]{0:T(128)} %bitcast.5, s32[1]{0:T(128)} %bitcast.6, s32[1]{0:T(128)} %bitcast.7), dimensions={0} | concatenate | bytes 64 | tf_op jit(solution)/shard_map/stack | solution.py:200
  33.6 0.0 collective-permute-done.5.refs_3_
  33.6 0.0 collective-permute-done.6.refs_4_
  33.6 0.0 collective-permute-done.7.refs_5_
  33.6 2.1 %collective-permute-done.8.refs_6_ = f32[4,8,256]{2,1,0:T(8,128)S(1)} collective-permute-done((f32[4,8,256]{2,1,0:T(8,128)S(1)}, f32[4,8,256]{2,1,0:T(8,128)S(1)}, u32[]{:S(2)}, u32[]{:S(2)}) %collective-permute-start.8) | collective-permute-done | bytes 32800 | tf_op jit(solution)/shard_map/ppermute | solution.py:199
  35.7 2.4 %collective-permute-done.9.refs_7_ = f32[4,8,256]{2,1,0:T(8,128)S(1)} collective-permute-done((f32[4,8,256]{2,1,0:T(8,128)S(1)}, f32[4,8,256]{2,1,0:T(8,128)S(1)}, u32[]{:S(2)}, u32[]{:S(2)}) %collective-permute-start.9) | collective-permute-done | bytes 32800 | tf_op jit(solution)/shard_map/ppermute | solution.py:199
  38.1 1.4 %assemble.1 = f32[4,8,2048]{2,1,0:T(8,128)} custom-call(s32[8]{0:T(128)} %stack.58.tiles_ref, f32[4,8,256]{2,1,0:T(8,128)S(1)} %get-tuple-element.12.refs_0_, f32[4,8,256]{2,1,0:T(8,128)S(1)} %collective-permute-done.3.refs_1_, f32[4,8,256]{2,1,0:T(8,128)S(1)} %collective-permute-done.4.refs_2_, f32[4,8,256]{2,1,0:T(8,128)S(1)} %collective-permute-done.5.refs_3_, ...), custom_call_target="tpu_custom_call" | custom-call | tf_op jit(solution)/shard_map/assemble/pallas_call | solution.py:160
  (2 shorter events, 0.0 us)
Async XLA Ops:
  0.0 18.4 %copy-start = (s32[8,4]{0,1:T(4,128)S(1)}, s32[8,4]{0,1:T(4,128)}, u32[]{:S(2)}) copy-start(s32[8,4]{0,1:T(4,128)} %param.7) | copy-start | bytes 388
  4.3 15.5 %collective-permute-start = (f32[4,64,256]{2,1,0:T(8,128)S(1)}, f32[4,64,256]{2,1,0:T(8,128)S(1)}, u32[]{:S(2)}, u32[]{:S(2)}) collective-permute-start(f32[4,64,256]{2,1,0:T(8,128)S(1)} %render_block.5), channel_id=1, source_target_pairs={{0,8},{8,0},{16,24},{24,16},{1,9},{9,1},{17,25},{25,17},{2,10},{10... | collective-permute-start | bytes 786440 | tf_op jit(solution)/shard_map/ppermute | solution.py:188
  10.5 13.4 %collective-permute-start.1 = (f32[4,64,256]{2,1,0:T(8,128)S(1)}, f32[4,64,256]{2,1,0:T(8,128)S(1)}, u32[]{:S(2)}, u32[]{:S(2)}) collective-permute-start(f32[4,64,256]{2,1,0:T(8,128)S(1)} %render_block.6), channel_id=1, source_target_pairs={{0,16},{8,24},{16,0},{24,8},{1,17},{9,25},{17,1},{25,9},{2,18},{10... | collective-permute-start | bytes 786440 | tf_op jit(solution)/shard_map/ppermute | solution.py:188
  15.1 8.8 %collective-permute-start.2 = (f32[4,64,256]{2,1,0:T(8,128)S(1)}, f32[4,64,256]{2,1,0:T(8,128)S(1)}, u32[]{:S(2)}, u32[]{:S(2)}) collective-permute-start(f32[4,64,256]{2,1,0:T(8,128)S(1)} %render_block.7), channel_id=1, source_target_pairs={{0,24},{8,16},{16,8},{24,0},{1,25},{9,17},{17,9},{25,1},{2,26},{10... | collective-permute-start | bytes 786440 | tf_op jit(solution)/shard_map/ppermute | solution.py:188
  24.8 4.5 %collective-permute-start.3 = (f32[4,8,256]{2,1,0:T(8,128)S(1)}, f32[4,8,256]{2,1,0:T(8,128)S(1)}, u32[]{:S(2)}, u32[]{:S(2)}) collective-permute-start(f32[4,8,256]{2,1,0:T(8,128)S(1)} %get-tuple-element.11), channel_id=1, source_target_pairs={{0,1},{1,0},{2,3},{3,2},{4,5},{5,4},{6,7},{7,6},{8,9},{9,8},{10,11... | collective-permute-start | bytes 98312 | tf_op jit(solution)/shard_map/ppermute | solution.py:199
  24.9 8.1 %collective-permute-start.4 = (f32[4,8,256]{2,1,0:T(8,128)S(1)}, f32[4,8,256]{2,1,0:T(8,128)S(1)}, u32[]{:S(2)}, u32[]{:S(2)}) collective-permute-start(f32[4,8,256]{2,1,0:T(8,128)S(1)} %get-tuple-element.10), channel_id=1, source_target_pairs={{0,2},{1,3},{2,0},{3,1},{4,6},{5,7},{6,4},{7,5},{8,10},{9,11},{10,... | collective-permute-start | bytes 98312 | tf_op jit(solution)/shard_map/ppermute | solution.py:199
  26.5 7.1 %collective-permute-start.5 = (f32[4,8,256]{2,1,0:T(8,128)S(1)}, f32[4,8,256]{2,1,0:T(8,128)S(1)}, u32[]{:S(2)}, u32[]{:S(2)}) collective-permute-start(f32[4,8,256]{2,1,0:T(8,128)S(1)} %get-tuple-element.9), channel_id=1, source_target_pairs={{0,3},{1,2},{2,1},{3,0},{4,7},{5,6},{6,5},{7,4},{8,11},{9,10},{10,... | collective-permute-start | bytes 98312 | tf_op jit(solution)/shard_map/ppermute | solution.py:199
  26.7 6.9 %collective-permute-start.6 = (f32[4,8,256]{2,1,0:T(8,128)S(1)}, f32[4,8,256]{2,1,0:T(8,128)S(1)}, u32[]{:S(2)}, u32[]{:S(2)}) collective-permute-start(f32[4,8,256]{2,1,0:T(8,128)S(1)} %get-tuple-element.8), channel_id=1, source_target_pairs={{0,4},{1,5},{2,6},{3,7},{4,0},{5,1},{6,2},{7,3},{8,12},{9,13},{10,... | collective-permute-start | bytes 98312 | tf_op jit(solution)/shard_map/ppermute | solution.py:199
  29.3 4.3 %collective-permute-start.7 = (f32[4,8,256]{2,1,0:T(8,128)S(1)}, f32[4,8,256]{2,1,0:T(8,128)S(1)}, u32[]{:S(2)}, u32[]{:S(2)}) collective-permute-start(f32[4,8,256]{2,1,0:T(8,128)S(1)} %get-tuple-element.7), channel_id=1, source_target_pairs={{0,5},{1,4},{2,7},{3,6},{4,1},{5,0},{6,3},{7,2},{8,13},{9,12},{10,... | collective-permute-start | bytes 98312 | tf_op jit(solution)/shard_map/ppermute | solution.py:199
  29.3 6.4 %collective-permute-start.8 = (f32[4,8,256]{2,1,0:T(8,128)S(1)}, f32[4,8,256]{2,1,0:T(8,128)S(1)}, u32[]{:S(2)}, u32[]{:S(2)}) collective-permute-start(f32[4,8,256]{2,1,0:T(8,128)S(1)} %get-tuple-element.6), channel_id=1, source_target_pairs={{0,6},{1,7},{2,4},{3,5},{4,2},{5,3},{6,0},{7,1},{8,14},{9,15},{10,... | collective-permute-start | bytes 98312 | tf_op jit(solution)/shard_map/ppermute | solution.py:199
  32.9 5.2 %collective-permute-start.9 = (f32[4,8,256]{2,1,0:T(8,128)S(1)}, f32[4,8,256]{2,1,0:T(8,128)S(1)}, u32[]{:S(2)}, u32[]{:S(2)}) collective-permute-start(f32[4,8,256]{2,1,0:T(8,128)S(1)} %get-tuple-element.5), channel_id=1, source_target_pairs={{0,7},{1,6},{2,5},{3,4},{4,3},{5,2},{6,1},{7,0},{8,15},{9,14},{10,... | collective-permute-start | bytes 98312 | tf_op jit(solution)/shard_map/ppermute | solution.py:199

commit v2 on v1

v2 whole, which is shorter than its diff:
```python
import functools

import jax
import jax.numpy as jnp
from jax import lax
from jax.experimental import pallas as pl
from jax.experimental.pallas import tpu as pltpu
from jax.sharding import PartitionSpec as P


extinction = 3.0
lanes = 128
sublanes = 8


def partner_of(index, step, count):
    if count & (count - 1) == 0:
        return index ^ step
    return (index + step) % count


def source_of(index, step, count):
    if count & (count - 1) == 0:
        return index ^ step
    return (index - step) % count


def in_vmem(array):
    return pltpu.with_memory_space_constraint(array, pltpu.VMEM)


def march(tables, bins_ref, first_row, out_ref):
    samples_here, _, col_count = bins_ref.shape
    row_count = out_ref.shape[1]
    halves = len(tables[0])
    groups = row_count // sublanes
    unrolled = 4 if groups % 4 == 0 else 1

    def advance(step, ignored):
        for inner in range(unrolled):
            row = pl.multiple_of((step * unrolled + inner) * sublanes, sublanes)
            to_rows = pl.ds(row, sublanes)
            rows = pl.ds(pl.multiple_of(first_row + row, sublanes), sublanes)
            for col in range(0, col_count, lanes):
                cols = slice(col, col + lanes)
                for sample in range(samples_here):
                    index = bins_ref[sample, rows, cols]
                    low = index & (lanes - 1)
                    high = index // lanes if halves > 2 else index >= lanes
                    picked = []
                    for c in range(4):
                        value = jnp.take_along_axis(
                            tables[c][0], low, axis=1, mode="promise_in_bounds"
                        )
                        for h in range(1, halves):
                            other = jnp.take_along_axis(
                                tables[c][h], low, axis=1, mode="promise_in_bounds"
                            )
                            value = jnp.where(high if halves == 2 else high == h, other, value)
                        picked.append(value)
                    if sample == 0:
                        sums = picked[:3]
                        through = picked[3]
                    else:
                        sums = [s + through * v for s, v in zip(sums, picked[:3])]
                        through = through * picked[3]
                for c in range(3):
                    out_ref[c, to_rows, cols] = sums[c]
                out_ref[3, to_rows, cols] = 1.0 - through
        return ignored

    lax.fori_loop(0, groups // unrolled, advance, 0)


def render_kernel(colors_hbm, opacity_hbm, bins_hbm, *refs, steps, rate):
    out_refs = refs[:-5]
    colors_ref, opacity_ref, bins_ref, bins_sems, table_sems = refs[-5:]
    block_rows = out_refs[0].shape[1]
    depth_count = lax.axis_size("depth")
    depth_index = lax.axis_index("depth")
    small = [
        pltpu.make_async_copy(colors_hbm, colors_ref, table_sems.at[0]),
        pltpu.make_async_copy(opacity_hbm, opacity_ref, table_sems.at[1]),
    ]
    for copy in small:
        copy.start()
    copies = []
    for i, step in enumerate(steps):
        first_row = partner_of(depth_index, step, depth_count) * block_rows
        rows = pl.ds(pl.multiple_of(first_row, block_rows), block_rows)
        to_rows = pl.ds(i * block_rows, block_rows)
        copies.append(
            pltpu.make_async_copy(bins_hbm.at[:, rows], bins_ref.at[:, to_rows], bins_sems.at[i])
        )
        copies[-1].start()
    for copy in small:
        copy.wait()
    opacity = opacity_ref[...].astype(jnp.float32).reshape(1, -1)
    clear = jnp.exp(-rate * opacity)
    shade = (1.0 - clear) * colors_ref[...].astype(jnp.float32)
    full = jnp.concatenate([shade, clear], axis=0)
    tables = [
        [
            jnp.broadcast_to(full[c : c + 1, h : h + lanes], (sublanes, lanes))
            for h in range(0, full.shape[1], lanes)
        ]
        for c in range(4)
    ]
    for i, copy in enumerate(copies):
        copy.wait()
        march(tables, bins_ref, i * block_rows, out_refs[i])


def smem_spec():
    return pl.BlockSpec(memory_space=pltpu.SMEM)


def vmem_spec():
    return pl.BlockSpec(memory_space=pltpu.VMEM)


def render(voxel_bins, colors, opacity, steps, block_rows, rate):
    samples_here, _, col_count = voxel_bins.shape
    return pl.pallas_call(
        functools.partial(render_kernel, steps=steps, rate=rate),
        out_shape=[pltpu.VMEM((4, block_rows, col_count), jnp.float32)] * len(steps),
        in_specs=[pl.BlockSpec(memory_space=pl.ANY)] * 3,
        out_specs=[vmem_spec()] * len(steps),
        scratch_shapes=[
            pltpu.VMEM(colors.shape, colors.dtype),
            pltpu.VMEM(opacity.shape, opacity.dtype),
            pltpu.VMEM((samples_here, len(steps) * block_rows, col_count), voxel_bins.dtype),
            pltpu.SemaphoreType.DMA((len(steps),)),
            pltpu.SemaphoreType.DMA((2,)),
        ],
        name="render",
    )(colors, opacity, voxel_bins)


def composite_kernel(order_ref, *refs):
    pieces, out_ref = refs[:-1], refs[-1]
    count = len(pieces)
    depth_index = lax.axis_index("depth")
    screen_index = lax.axis_index("screen")
    places = [
        order_ref[screen_index, source_of(depth_index, step, count)] for step in range(count)
    ]
    target_count, _, owned_rows, _ = out_ref.shape
    together = max(1, sublanes // owned_rows)
    group_rows = together * owned_rows

    def advance(group, ignored):
        rows = pl.ds(pl.multiple_of(group * group_rows, group_rows), group_rows)

        def put(channel, value):
            for i in range(together):
                out_ref[group * together + i, channel] = value[
                    i * owned_rows : (i + 1) * owned_rows
                ]

        clear = [1.0 - piece[3, rows, :] for piece in pieces]
        before = [None] * count
        for j in range(count):
            for k in range(j + 1, count):
                first = places[j] < places[k]
                onto_k = jnp.where(first, clear[j], 1.0)
                onto_j = jnp.where(first, 1.0, clear[k])
                before[k] = onto_k if before[k] is None else before[k] * onto_k
                before[j] = onto_j if before[j] is None else before[j] * onto_j
        for c in range(3):
            total = before[0] * pieces[0][c, rows, :]
            for j in range(1, count):
                total = total + before[j] * pieces[j][c, rows, :]
            put(c, total)
        through = clear[0]
        for j in range(1, count):
            through = through * clear[j]
        put(3, 1.0 - through)
        return ignored

    lax.fori_loop(0, target_count // together, advance, 0)


def composite(pieces, slab_order, target_count):
    _, block_rows, col_count = pieces[0].shape
    return pl.pallas_call(
        composite_kernel,
        out_shape=pltpu.VMEM(
            (target_count, 4, block_rows // target_count, col_count), jnp.float32
        ),
        in_specs=[smem_spec()] + [vmem_spec()] * len(pieces),
        out_specs=vmem_spec(),
        name="composite",
    )(slab_order, *[in_vmem(piece) for piece in pieces])


def assemble_kernel(*refs, steps):
    parts, out_ref, sems = refs[:-2], refs[-2], refs[-1]
    col_count = parts[0].shape[-1]
    screen_count = lax.axis_size("screen")
    screen_index = lax.axis_index("screen")
    copies = []
    for i, part in enumerate(parts):
        tile = source_of(screen_index, steps[i], screen_count)
        cols = pl.ds(pl.multiple_of(tile * col_count, col_count), col_count)
        copies.append(pltpu.make_async_copy(part, out_ref.at[:, :, cols], sems.at[i]))
        copies[-1].start()
    for copy in copies:
        copy.wait()


def assemble(parts, steps):
    channels, owned_rows, col_count = parts[0].shape
    return pl.pallas_call(
        functools.partial(assemble_kernel, steps=steps),
        out_shape=jax.ShapeDtypeStruct(
            (channels, owned_rows, col_count * len(parts)), jnp.float32
        ),
        in_specs=[vmem_spec()] * len(parts),
        out_specs=pl.BlockSpec(memory_space=pl.ANY),
        scratch_shapes=[pltpu.SemaphoreType.DMA((len(parts),))],
        name="assemble",
    )(*[in_vmem(part) for part in parts])


def local(voxel_bins, colors, opacity, slab_order):
    depth_count = lax.axis_size("depth")
    screen_count = lax.axis_size("screen")
    samples_here, row_count, _ = voxel_bins.shape
    rate = extinction / (samples_here * depth_count)
    screen_index = lax.axis_index("screen")
    block_rows = row_count // depth_count
    pieces = [None] * depth_count
    for steps in ((1, 2), tuple(range(3, depth_count)), (0,)):
        rendered = render(voxel_bins, colors, opacity, steps, block_rows, rate)
        for step, piece in zip(steps, rendered):
            if step:
                pairs = [(i, partner_of(i, step, depth_count)) for i in range(depth_count)]
                piece = lax.ppermute(piece, "depth", pairs)
            pieces[step] = piece
    blocks = composite(pieces, slab_order, screen_count)
    parts = []
    steps = list(range(screen_count - 1, 0, -1)) + [0]
    for step in steps:
        target = partner_of(screen_index, step, screen_count)
        part = lax.dynamic_index_in_dim(blocks, target, 0, keepdims=False)
        if step:
            pairs = [(i, partner_of(i, step, screen_count)) for i in range(screen_count)]
            part = lax.ppermute(part, "screen", pairs)
        parts.append(part)
    return assemble(parts, tuple(steps))


def solution(mesh):
    placed = (P("depth", None, "screen"), P(), P(), P())
    return jax.shard_map(
        local,
        mesh=mesh,
        in_specs=placed,
        out_specs=P(None, ("depth", "screen"), None),
        check_vma=False,
    )
```

time: 39.7 us -> 34.2 us (0.86)
  Pallas kernels: 14.6 us -> 11.5 us
  local copies, waits for them, and re-layouts: 3.18 us -> 0.71 us
    pallas_call x5 -> x4, Pallas kernels: 13.8 us -> 10.6 us  [the longest x3 9.87 us: render(): pl.pallas_call(functools.partial(render_kernel, steps=steps, rate=rate),...]
    ppermute x3, waiting for transfers between devices: 4.11 us -> 5.58 us  [local(): piece = lax.ppermute(piece, 'depth', pairs)]
    ppermute x7, waiting for transfers between devices: 4.48 us -> 3.11 us  [local(): part = lax.ppermute(part, 'screen', pairs)]
    broadcast_in_dim x1 -> x0, local copies, waits for them, and re-layouts: 1.23 us -> none  [local(): opacity_row = opacity[None]]
    gather x1 -> x0, local copies, waits for them, and re-layouts: 1.15 us -> none  [local(): places = own_order[sources]]
    unnamed x2 -> x3, local copies, waits for them, and re-layouts: 0.01 us -> 0.68 us
    another operation x1 -> x0, local copies, waits for them, and re-layouts: 0.57 us -> none  [local(): jnp.stack([source_of(screen_index, step, screen_count) for step in range(...]
  transfers between devices with their start and end apart: 10 -> 10, of which waited for: 3 -> 4; matrix products, arithmetic and copies ran while one was open for 5% -> 2% of each run, Pallas kernels for 24% -> 16%
where the time goes in v2:
time: 34.2 us; the launch traced here: 34 us
  starting transfers between devices  13 us (38%)
  Pallas kernels  11.5 us (34%)
  waiting for transfers between devices  8.69 us (25%)
  local copies, waits for them, and re-layouts  0.71 us (2%)
    pallas_call x3, Pallas kernels, render(): pl.pallas_call(functools.partial(render_kernel, steps=steps, rate=rate),...  9.87 us
    ppermute x7, starting transfers between devices, local(): part = lax.ppermute(part, 'screen', pairs)  8.34 us
    ppermute x3, waiting for transfers between devices, local(): piece = lax.ppermute(piece, 'depth', pairs)  5.58 us
    ppermute x3, starting transfers between devices, local(): piece = lax.ppermute(piece, 'depth', pairs)  4.65 us
    ppermute x7, waiting for transfers between devices, local(): part = lax.ppermute(part, 'screen', pairs)  3.11 us
    pallas_call x1, Pallas kernels, composite(): pl.pallas_call(composite_kernel, out_shape=pltpu.VMEM((target_count, 4, b...  0.91 us
    pallas_call x1, Pallas kernels, assemble(): pl.pallas_call(functools.partial(assemble_kernel, steps=steps), out_shape...  0.76 us
  transfers between devices with their start and end apart: 10, of which 4 were waited for; matrix products, arithmetic and copies ran while one was open for 2% of the time, Pallas kernels for 16%

profile of v2, /device:TPU:0, one launch (start us, length us, event | category | flops | bytes accessed | tf_op | source)
XLA Modules:
  0.0 34.0 jit_solution(15013233918360331896)
XLA Ops:
  0.0 4.4 %render.4 = (f32[4,64,256]{2,1,0:T(8,128)S(1)}, f32[4,64,256]{2,1,0:T(8,128)S(1)}) custom-call(bf16[3,256]{1,0:T(4,128)(2,1)} %colors_hbm.5, bf16[256]{0:T(256)(128)(2,1)} %opacity_hbm.5, s32[8,256,256]{2,1,0:T(8,128)} %bins_hbm.5), custom_call_target="tpu_custom_call" | custom-call | tf_op jit(solution)/shard_map/render/pallas_call | solution.py:124
  4.4 3.0 %collective-permute-start = (f32[4,64,256]{2,1,0:T(8,128)S(1)}, f32[4,64,256]{2,1,0:T(8,128)S(1)}, u32[]{:S(2)}, u32[]{:S(2)}) collective-permute-start(f32[4,64,256]{2,1,0:T(8,128)S(1)} %get-tuple-element.7), channel_id=1, source_target_pairs={{0,8},{8,0},{16,24},{24,16},{1,9},{9,1},{17,25},{25,17},{2,10},{10... | collective-permute-start | bytes 786440 | tf_op jit(solution)/shard_map/ppermute | solution.py:239
  7.4 0.0 copy-start
  7.4 1.5 %collective-permute-start.1 = (f32[4,64,256]{2,1,0:T(8,128)S(1)}, f32[4,64,256]{2,1,0:T(8,128)S(1)}, u32[]{:S(2)}, u32[]{:S(2)}) collective-permute-start(f32[4,64,256]{2,1,0:T(8,128)S(1)} %get-tuple-element.8), channel_id=1, source_target_pairs={{0,16},{8,24},{16,0},{24,8},{1,17},{9,25},{17,1},{25,9},{2,18},{10... | collective-permute-start | bytes 786440 | tf_op jit(solution)/shard_map/ppermute | solution.py:239
  8.9 2.7 %render.5 = f32[4,64,256]{2,1,0:T(8,128)S(1)} custom-call(bf16[3,256]{1,0:T(4,128)(2,1)} %colors_hbm.5, bf16[256]{0:T(256)(128)(2,1)} %opacity_hbm.5, s32[8,256,256]{2,1,0:T(8,128)} %bins_hbm.5), custom_call_target="tpu_custom_call" | custom-call | tf_op jit(solution)/shard_map/render/pallas_call | solution.py:124
  11.7 0.1 collective-permute-start.2
  11.8 2.7 %render.3.refs_0_ = f32[4,64,256]{2,1,0:T(8,128)S(1)} custom-call(bf16[3,256]{1,0:T(4,128)(2,1)} %colors_hbm.5, bf16[256]{0:T(256)(128)(2,1)} %opacity_hbm.5, s32[8,256,256]{2,1,0:T(8,128)} %bins_hbm.5), custom_call_target="tpu_custom_call" | custom-call | tf_op jit(solution)/shard_map/render/pallas_call | solution.py:124
  14.6 0.0 copy-done
  14.6 0.7 %copy.5.order_ref = s32[8,4]{1,0:T(8,128)} copy(s32[8,4]{0,1:T(4,128)S(1)} %copy-done) | data formatting | bytes 256 | tf_op args[3]
  15.2 0.0 collective-permute-done.refs_1_
  15.2 5.6 %collective-permute-done.1.refs_2_ = f32[4,64,256]{2,1,0:T(8,128)S(1)} collective-permute-done((f32[4,64,256]{2,1,0:T(8,128)S(1)}, f32[4,64,256]{2,1,0:T(8,128)S(1)}, u32[]{:S(2)}, u32[]{:S(2)}) %collective-permute-start.1) | collective-permute-done | bytes 262176 | tf_op jit(solution)/shard_map/ppermute | solution.py:239
  20.8 0.0 collective-permute-done.2.refs_3_
  20.8 0.9 %composite.1 = f32[8,4,8,256]{3,2,1,0:T(8,128)S(1)} custom-call(s32[8,4]{1,0:T(8,128)} %copy.5.order_ref, f32[4,64,256]{2,1,0:T(8,128)S(1)} %render.3.refs_0_, f32[4,64,256]{2,1,0:T(8,128)S(1)} %collective-permute-done.refs_1_, f32[4,64,256]{2,1,0:T(8,128)S(1)} %collective-permute-done.1.refs_2_, f32[4,64,256]{2,1,0:T(8,128)S(1)} %collective-permute-done.2.refs_3_), custom_call_target="tpu_custom_call" | custom-call | tf_op jit(solution)/shard_map/composite/pallas_call | solution.py:186
  21.8 1.9 %collective-permute-start.3 = (f32[4,8,256]{2,1,0:T(8,128)S(1)}, f32[4,8,256]{2,1,0:T(8,128)S(1)}, u32[]{:S(2)}, u32[]{:S(2)}) collective-permute-start(f32[4,8,256]{2,1,0:T(8,128)S(1)} %get-tuple-element.16), channel_id=1, source_target_pairs={{0,7},{1,6},{2,5},{3,4},{4,3},{5,2},{6,1},{7,0},{8,15},{9,14},{10,... | collective-permute-start | bytes 98312 | tf_op jit(solution)/shard_map/ppermute | solution.py:249
  23.7 1.9 %collective-permute-start.4 = (f32[4,8,256]{2,1,0:T(8,128)S(1)}, f32[4,8,256]{2,1,0:T(8,128)S(1)}, u32[]{:S(2)}, u32[]{:S(2)}) collective-permute-start(f32[4,8,256]{2,1,0:T(8,128)S(1)} %get-tuple-element.15), channel_id=1, source_target_pairs={{0,6},{1,7},{2,4},{3,5},{4,2},{5,3},{6,0},{7,1},{8,14},{9,15},{10,... | collective-permute-start | bytes 98312 | tf_op jit(solution)/shard_map/ppermute | solution.py:249
  25.5 0.4 %collective-permute-start.5 = (f32[4,8,256]{2,1,0:T(8,128)S(1)}, f32[4,8,256]{2,1,0:T(8,128)S(1)}, u32[]{:S(2)}, u32[]{:S(2)}) collective-permute-start(f32[4,8,256]{2,1,0:T(8,128)S(1)} %get-tuple-element.14), channel_id=1, source_target_pairs={{0,5},{1,4},{2,7},{3,6},{4,1},{5,0},{6,3},{7,2},{8,13},{9,12},{10,... | collective-permute-start | bytes 98312 | tf_op jit(solution)/shard_map/ppermute | solution.py:249
  25.9 2.2 %collective-permute-start.6 = (f32[4,8,256]{2,1,0:T(8,128)S(1)}, f32[4,8,256]{2,1,0:T(8,128)S(1)}, u32[]{:S(2)}, u32[]{:S(2)}) collective-permute-start(f32[4,8,256]{2,1,0:T(8,128)S(1)} %get-tuple-element.13), channel_id=1, source_target_pairs={{0,4},{1,5},{2,6},{3,7},{4,0},{5,1},{6,2},{7,3},{8,12},{9,13},{10,... | collective-permute-start | bytes 98312 | tf_op jit(solution)/shard_map/ppermute | solution.py:249
  28.1 0.9 %collective-permute-start.7 = (f32[4,8,256]{2,1,0:T(8,128)S(1)}, f32[4,8,256]{2,1,0:T(8,128)S(1)}, u32[]{:S(2)}, u32[]{:S(2)}) collective-permute-start(f32[4,8,256]{2,1,0:T(8,128)S(1)} %get-tuple-element.12), channel_id=1, source_target_pairs={{0,3},{1,2},{2,1},{3,0},{4,7},{5,6},{6,5},{7,4},{8,11},{9,10},{10,... | collective-permute-start | bytes 98312 | tf_op jit(solution)/shard_map/ppermute | solution.py:249
  29.0 0.0 collective-permute-done.3.refs_0_
  29.0 0.9 %collective-permute-start.8 = (f32[4,8,256]{2,1,0:T(8,128)S(1)}, f32[4,8,256]{2,1,0:T(8,128)S(1)}, u32[]{:S(2)}, u32[]{:S(2)}) collective-permute-start(f32[4,8,256]{2,1,0:T(8,128)S(1)} %get-tuple-element.11), channel_id=1, source_target_pairs={{0,2},{1,3},{2,0},{3,1},{4,6},{5,7},{6,4},{7,5},{8,10},{9,11},{10,... | collective-permute-start | bytes 98312 | tf_op jit(solution)/shard_map/ppermute | solution.py:249
  29.9 0.0 collective-permute-done.4.refs_1_
  29.9 0.2 collective-permute-start.9
  30.1 1.3 %collective-permute-done.5.refs_2_ = f32[4,8,256]{2,1,0:T(8,128)S(1)} collective-permute-done((f32[4,8,256]{2,1,0:T(8,128)S(1)}, f32[4,8,256]{2,1,0:T(8,128)S(1)}, u32[]{:S(2)}, u32[]{:S(2)}) %collective-permute-start.5) | collective-permute-done | bytes 32800 | tf_op jit(solution)/shard_map/ppermute | solution.py:249
  31.5 0.8 %collective-permute-done.6.refs_3_ = f32[4,8,256]{2,1,0:T(8,128)S(1)} collective-permute-done((f32[4,8,256]{2,1,0:T(8,128)S(1)}, f32[4,8,256]{2,1,0:T(8,128)S(1)}, u32[]{:S(2)}, u32[]{:S(2)}) %collective-permute-start.6) | collective-permute-done | bytes 32800 | tf_op jit(solution)/shard_map/ppermute | solution.py:249
  32.3 0.0 collective-permute-done.7.refs_4_
  32.3 1.0 %collective-permute-done.8.refs_5_ = f32[4,8,256]{2,1,0:T(8,128)S(1)} collective-permute-done((f32[4,8,256]{2,1,0:T(8,128)S(1)}, f32[4,8,256]{2,1,0:T(8,128)S(1)}, u32[]{:S(2)}, u32[]{:S(2)}) %collective-permute-start.8) | collective-permute-done | bytes 32800 | tf_op jit(solution)/shard_map/ppermute | solution.py:249
  33.2 0.0 collective-permute-done.9.refs_6_
  33.2 0.8 %assemble.1 = f32[4,8,2048]{2,1,0:T(8,128)} custom-call(f32[4,8,256]{2,1,0:T(8,128)S(1)} %collective-permute-done.3.refs_0_, f32[4,8,256]{2,1,0:T(8,128)S(1)} %collective-permute-done.4.refs_1_, f32[4,8,256]{2,1,0:T(8,128)S(1)} %collective-permute-done.5.refs_2_, f32[4,8,256]{2,1,0:T(8,128)S(1)} %collective-permute-done.6.refs_3_, ...), custom_call_target="tpu_custom_call" | custom-call | tf_op jit(solution)/shard_map/assemble/pallas_call | solution.py:214
  (1 shorter events, 0.0 us)
Async XLA Ops:
  4.4 10.8 %collective-permute-start = (f32[4,64,256]{2,1,0:T(8,128)S(1)}, f32[4,64,256]{2,1,0:T(8,128)S(1)}, u32[]{:S(2)}, u32[]{:S(2)}) collective-permute-start(f32[4,64,256]{2,1,0:T(8,128)S(1)} %get-tuple-element.7), channel_id=1, source_target_pairs={{0,8},{8,0},{16,24},{24,16},{1,9},{9,1},{17,25},{25,17},{2,10},{10... | collective-permute-start | bytes 786440 | tf_op jit(solution)/shard_map/ppermute | solution.py:239
  7.4 7.1 %copy-start = (s32[8,4]{0,1:T(4,128)S(1)}, s32[8,4]{0,1:T(4,128)}, u32[]{:S(2)}) copy-start(s32[8,4]{0,1:T(4,128)} %param.7) | copy-start | bytes 388
  7.4 13.4 %collective-permute-start.1 = (f32[4,64,256]{2,1,0:T(8,128)S(1)}, f32[4,64,256]{2,1,0:T(8,128)S(1)}, u32[]{:S(2)}, u32[]{:S(2)}) collective-permute-start(f32[4,64,256]{2,1,0:T(8,128)S(1)} %get-tuple-element.8), channel_id=1, source_target_pairs={{0,16},{8,24},{16,0},{24,8},{1,17},{9,25},{17,1},{25,9},{2,18},{10... | collective-permute-start | bytes 786440 | tf_op jit(solution)/shard_map/ppermute | solution.py:239
  11.7 9.1 %collective-permute-start.2 = (f32[4,64,256]{2,1,0:T(8,128)S(1)}, f32[4,64,256]{2,1,0:T(8,128)S(1)}, u32[]{:S(2)}, u32[]{:S(2)}) collective-permute-start(f32[4,64,256]{2,1,0:T(8,128)S(1)} %render.5), channel_id=1, source_target_pairs={{0,24},{8,16},{16,8},{24,0},{1,25},{9,17},{17,9},{25,1},{2,26},{10... | collective-permute-start | bytes 786440 | tf_op jit(solution)/shard_map/ppermute | solution.py:239
  21.8 7.2 %collective-permute-start.3 = (f32[4,8,256]{2,1,0:T(8,128)S(1)}, f32[4,8,256]{2,1,0:T(8,128)S(1)}, u32[]{:S(2)}, u32[]{:S(2)}) collective-permute-start(f32[4,8,256]{2,1,0:T(8,128)S(1)} %get-tuple-element.16), channel_id=1, source_target_pairs={{0,7},{1,6},{2,5},{3,4},{4,3},{5,2},{6,1},{7,0},{8,15},{9,14},{10,... | collective-permute-start | bytes 98312 | tf_op jit(solution)/shard_map/ppermute | solution.py:249
  23.7 6.3 %collective-permute-start.4 = (f32[4,8,256]{2,1,0:T(8,128)S(1)}, f32[4,8,256]{2,1,0:T(8,128)S(1)}, u32[]{:S(2)}, u32[]{:S(2)}) collective-permute-start(f32[4,8,256]{2,1,0:T(8,128)S(1)} %get-tuple-element.15), channel_id=1, source_target_pairs={{0,6},{1,7},{2,4},{3,5},{4,2},{5,3},{6,0},{7,1},{8,14},{9,15},{10,... | collective-permute-start | bytes 98312 | tf_op jit(solution)/shard_map/ppermute | solution.py:249
  25.5 5.9 %collective-permute-start.5 = (f32[4,8,256]{2,1,0:T(8,128)S(1)}, f32[4,8,256]{2,1,0:T(8,128)S(1)}, u32[]{:S(2)}, u32[]{:S(2)}) collective-permute-start(f32[4,8,256]{2,1,0:T(8,128)S(1)} %get-tuple-element.14), channel_id=1, source_target_pairs={{0,5},{1,4},{2,7},{3,6},{4,1},{5,0},{6,3},{7,2},{8,13},{9,12},{10,... | collective-permute-start | bytes 98312 | tf_op jit(solution)/shard_map/ppermute | solution.py:249
  25.9 6.4 %collective-permute-start.6 = (f32[4,8,256]{2,1,0:T(8,128)S(1)}, f32[4,8,256]{2,1,0:T(8,128)S(1)}, u32[]{:S(2)}, u32[]{:S(2)}) collective-permute-start(f32[4,8,256]{2,1,0:T(8,128)S(1)} %get-tuple-element.13), channel_id=1, source_target_pairs={{0,4},{1,5},{2,6},{3,7},{4,0},{5,1},{6,2},{7,3},{8,12},{9,13},{10,... | collective-permute-start | bytes 98312 | tf_op jit(solution)/shard_map/ppermute | solution.py:249
  28.1 4.2 %collective-permute-start.7 = (f32[4,8,256]{2,1,0:T(8,128)S(1)}, f32[4,8,256]{2,1,0:T(8,128)S(1)}, u32[]{:S(2)}, u32[]{:S(2)}) collective-permute-start(f32[4,8,256]{2,1,0:T(8,128)S(1)} %get-tuple-element.12), channel_id=1, source_target_pairs={{0,3},{1,2},{2,1},{3,0},{4,7},{5,6},{6,5},{7,4},{8,11},{9,10},{10,... | collective-permute-start | bytes 98312 | tf_op jit(solution)/shard_map/ppermute | solution.py:249
  29.0 4.2 %collective-permute-start.8 = (f32[4,8,256]{2,1,0:T(8,128)S(1)}, f32[4,8,256]{2,1,0:T(8,128)S(1)}, u32[]{:S(2)}, u32[]{:S(2)}) collective-permute-start(f32[4,8,256]{2,1,0:T(8,128)S(1)} %get-tuple-element.11), channel_id=1, source_target_pairs={{0,2},{1,3},{2,0},{3,1},{4,6},{5,7},{6,4},{7,5},{8,10},{9,11},{10,... | collective-permute-start | bytes 98312 | tf_op jit(solution)/shard_map/ppermute | solution.py:249
  29.9 3.3 %collective-permute-start.9 = (f32[4,8,256]{2,1,0:T(8,128)S(1)}, f32[4,8,256]{2,1,0:T(8,128)S(1)}, u32[]{:S(2)}, u32[]{:S(2)}) collective-permute-start(f32[4,8,256]{2,1,0:T(8,128)S(1)} %get-tuple-element.10), channel_id=1, source_target_pairs={{0,1},{1,0},{2,3},{3,2},{4,5},{5,4},{6,7},{7,6},{8,9},{9,8},{10,11... | collective-permute-start | bytes 98312 | tf_op jit(solution)/shard_map/ppermute | solution.py:249

commit v3 on v2

v3 whole, which is shorter than its diff:
```python
import functools

import jax
import jax.numpy as jnp
from jax import lax
from jax.experimental import pallas as pl
from jax.experimental.pallas import tpu as pltpu
from jax.sharding import PartitionSpec as P


extinction = 3.0
lanes = 128
sublanes = 8


def partner_of(index, step, count):
    if count & (count - 1) == 0:
        return index ^ step
    return (index + step) % count


def source_of(index, step, count):
    if count & (count - 1) == 0:
        return index ^ step
    return (index - step) % count


def in_vmem(array):
    return pltpu.with_memory_space_constraint(array, pltpu.VMEM)


def march(tables, bins_ref, row, col):
    halves = len(tables[0])
    rows = pl.ds(row, sublanes)
    cols = slice(col, col + lanes)
    for sample in range(bins_ref.shape[0]):
        index = bins_ref[sample, rows, cols]
        low = index & (lanes - 1)
        high = index // lanes if halves > 2 else index >= lanes
        picked = []
        for c in range(4):
            value = jnp.take_along_axis(tables[c][0], low, axis=1, mode="promise_in_bounds")
            for h in range(1, halves):
                other = jnp.take_along_axis(tables[c][h], low, axis=1, mode="promise_in_bounds")
                value = jnp.where(high if halves == 2 else high == h, other, value)
            picked.append(value)
        if sample == 0:
            sums = picked[:3]
            through = picked[3]
        else:
            sums = [s + through * v for s, v in zip(sums, picked[:3])]
            through = through * picked[3]
    return sums + [1.0 - through]


def march_block(tables, bins_ref, first_row, same_ref, other_ref, parity):
    pair_count, _, owned_rows, col_count = same_ref.shape
    outs = (same_ref, other_ref)

    def whole_groups(pair):
        for flip in range(2):
            target = 2 * pair + (parity ^ flip)
            for sub in range(0, owned_rows, sublanes):
                row = pl.multiple_of(first_row + target * owned_rows + sub, sublanes)
                for col in range(0, col_count, lanes):
                    values = march(tables, bins_ref, row, col)
                    for c in range(4):
                        outs[flip][pair, c, sub : sub + sublanes, col : col + lanes] = values[c]

    def shared_group(group):
        row = pl.multiple_of(first_row + group * sublanes, sublanes)
        pairs = sublanes // (2 * owned_rows)
        for col in range(0, col_count, lanes):
            values = march(tables, bins_ref, row, col)
            for c in range(4):
                for i in range(pairs):
                    start = 2 * i * owned_rows
                    even = values[c][start : start + owned_rows]
                    odd = values[c][start + owned_rows : start + 2 * owned_rows]
                    where = (group * pairs + i, c, slice(None), slice(col, col + lanes))
                    same_ref[where] = jnp.where(parity == 0, even, odd)
                    other_ref[where] = jnp.where(parity == 0, odd, even)

    if owned_rows % sublanes == 0:
        visit, count = whole_groups, pair_count
    else:
        visit, count = shared_group, 2 * pair_count * owned_rows // sublanes
    unrolled = 2 if count % 2 == 0 else 1

    def advance(step, ignored):
        for inner in range(unrolled):
            visit(step * unrolled + inner)
        return ignored

    lax.fori_loop(0, count // unrolled, advance, 0)


def render_kernel(colors_hbm, opacity_hbm, bins_hbm, *refs, steps, rate):
    out_refs = refs[:-5]
    colors_ref, opacity_ref, bins_ref, bins_sems, table_sems = refs[-5:]
    pair_count, ignored, owned_rows, ignored = out_refs[0].shape
    block_rows = 2 * pair_count * owned_rows
    parity = lax.axis_index("screen") % 2
    depth_count = lax.axis_size("depth")
    depth_index = lax.axis_index("depth")
    small = [
        pltpu.make_async_copy(colors_hbm, colors_ref, table_sems.at[0]),
        pltpu.make_async_copy(opacity_hbm, opacity_ref, table_sems.at[1]),
    ]
    for copy in small:
        copy.start()
    copies = []
    for i, step in enumerate(steps):
        first_row = partner_of(depth_index, step, depth_count) * block_rows
        rows = pl.ds(pl.multiple_of(first_row, block_rows), block_rows)
        to_rows = pl.ds(i * block_rows, block_rows)
        copies.append(
            pltpu.make_async_copy(bins_hbm.at[:, rows], bins_ref.at[:, to_rows], bins_sems.at[i])
        )
        copies[-1].start()
    for copy in small:
        copy.wait()
    opacity = opacity_ref[...].astype(jnp.float32).reshape(1, -1)
    clear = jnp.exp(-rate * opacity)
    shade = (1.0 - clear) * colors_ref[...].astype(jnp.float32)
    full = jnp.concatenate([shade, clear], axis=0)
    tables = [
        [
            jnp.broadcast_to(full[c : c + 1, h : h + lanes], (sublanes, lanes))
            for h in range(0, full.shape[1], lanes)
        ]
        for c in range(4)
    ]
    for i, copy in enumerate(copies):
        copy.wait()
        march_block(
            tables, bins_ref, i * block_rows, out_refs[2 * i], out_refs[2 * i + 1], parity
        )


def smem_spec():
    return pl.BlockSpec(memory_space=pltpu.SMEM)


def vmem_spec():
    return pl.BlockSpec(memory_space=pltpu.VMEM)


def render(voxel_bins, colors, opacity, steps, piece_shape, block_rows, rate):
    samples_here, _, col_count = voxel_bins.shape
    return pl.pallas_call(
        functools.partial(render_kernel, steps=steps, rate=rate),
        out_shape=[pltpu.VMEM(piece_shape, jnp.float32)] * (2 * len(steps)),
        in_specs=[pl.BlockSpec(memory_space=pl.ANY)] * 3,
        out_specs=[vmem_spec()] * (2 * len(steps)),
        scratch_shapes=[
            pltpu.VMEM(colors.shape, colors.dtype),
            pltpu.VMEM(opacity.shape, opacity.dtype),
            pltpu.VMEM((samples_here, len(steps) * block_rows, col_count), voxel_bins.dtype),
            pltpu.SemaphoreType.DMA((len(steps),)),
            pltpu.SemaphoreType.DMA((2,)),
        ],
        name="render",
    )(colors, opacity, voxel_bins)


def composite_kernel(order_ref, *refs):
    pieces, out_ref = refs[:-1], refs[-1]
    count = len(pieces) // 2
    col_count = out_ref.shape[3] // 2
    depth_index = lax.axis_index("depth")
    screen_index = lax.axis_index("screen")

    def advance(target, ignored):
        for side, tile in enumerate((screen_index, screen_index ^ 1)):
            own = pieces[side * count : (side + 1) * count]
            places = [
                order_ref[tile, source_of(depth_index, step, count)] for step in range(count)
            ]
            cols = pl.ds(pl.multiple_of((tile % 2) * col_count, col_count), col_count)
            clear = [1.0 - piece[target, 3] for piece in own]
            before = [None] * count
            for j in range(count):
                for k in range(j + 1, count):
                    first = places[j] < places[k]
                    onto_k = jnp.where(first, clear[j], 1.0)
                    onto_j = jnp.where(first, 1.0, clear[k])
                    before[k] = onto_k if before[k] is None else before[k] * onto_k
                    before[j] = onto_j if before[j] is None else before[j] * onto_j
            for c in range(3):
                total = before[0] * own[0][target, c]
                for j in range(1, count):
                    total = total + before[j] * own[j][target, c]
                out_ref[target, c, :, cols] = total
            through = clear[0]
            for j in range(1, count):
                through = through * clear[j]
            out_ref[target, 3, :, cols] = 1.0 - through
        return ignored

    lax.fori_loop(0, out_ref.shape[0], advance, 0)


def composite(pieces, slab_order):
    pair_count, channels, owned_rows, col_count = pieces[0].shape
    return pl.pallas_call(
        composite_kernel,
        out_shape=pltpu.VMEM((pair_count, channels, owned_rows, 2 * col_count), jnp.float32),
        in_specs=[smem_spec()] + [vmem_spec()] * len(pieces),
        out_specs=vmem_spec(),
        name="composite",
    )(slab_order, *[in_vmem(piece) for piece in pieces])


def assemble_kernel(*refs, steps):
    parts, out_ref, sems = refs[:-2], refs[-2], refs[-1]
    col_count = parts[0].shape[-1]
    pair_count = lax.axis_size("screen") // 2
    pair_index = lax.axis_index("screen") // 2
    copies = []
    for i, part in enumerate(parts):
        tile = source_of(pair_index, steps[i], pair_count)
        cols = pl.ds(pl.multiple_of(tile * col_count, col_count), col_count)
        copies.append(pltpu.make_async_copy(part, out_ref.at[:, :, cols], sems.at[i]))
        copies[-1].start()
    for copy in copies:
        copy.wait()


def assemble(parts, steps):
    channels, owned_rows, col_count = parts[0].shape
    return pl.pallas_call(
        functools.partial(assemble_kernel, steps=steps),
        out_shape=jax.ShapeDtypeStruct(
            (channels, owned_rows, col_count * len(parts)), jnp.float32
        ),
        in_specs=[vmem_spec()] * len(parts),
        out_specs=pl.BlockSpec(memory_space=pl.ANY),
        scratch_shapes=[pltpu.SemaphoreType.DMA((len(parts),))],
        name="assemble",
    )(*[in_vmem(part) for part in parts])


def local(voxel_bins, colors, opacity, slab_order):
    depth_count = lax.axis_size("depth")
    screen_count = lax.axis_size("screen")
    samples_here, row_count, col_count = voxel_bins.shape
    rate = extinction / (samples_here * depth_count)
    block_rows = row_count // depth_count
    pair_count = screen_count // 2
    piece_shape = (pair_count, 4, block_rows // screen_count, col_count)

    def exchange(piece, step, flip):
        pairs = [
            (
                d * screen_count + s,
                partner_of(d, step, depth_count) * screen_count + (s ^ flip),
            )
            for d in range(depth_count)
            for s in range(screen_count)
        ]
        return lax.ppermute(piece, ("depth", "screen"), pairs)

    same = [None] * depth_count
    other = [None] * depth_count
    for steps in ((1, 2), tuple(range(3, depth_count)), (0,)):
        rendered = render(voxel_bins, colors, opacity, steps, piece_shape, block_rows, rate)
        for i, step in enumerate(steps):
            same[step] = exchange(rendered[2 * i], step, 0) if step else rendered[2 * i]
            other[step] = exchange(rendered[2 * i + 1], step, 1)
    blocks = composite(same + other, slab_order)
    parts = []
    steps = list(range(pair_count - 1, 0, -1)) + [0]
    for step in steps:
        target = partner_of(lax.axis_index("screen") // 2, step, pair_count)
        part = lax.dynamic_index_in_dim(blocks, target, 0, keepdims=False)
        if step:
            pairs = [
                (s, partner_of(s // 2, step, pair_count) * 2 + s % 2) for s in range(screen_count)
            ]
            part = lax.ppermute(part, "screen", pairs)
        parts.append(part)
    return assemble(parts, tuple(steps))


def solution(mesh):
    placed = (P("depth", None, "screen"), P(), P(), P())
    return jax.shard_map(
        local,
        mesh=mesh,
        in_specs=placed,
        out_specs=P(None, ("depth", "screen"), None),
        check_vma=False,
    )
```

time: 34.2 us -> 36.5 us (1.067)
  waiting for transfers between devices: 8.69 us -> 11.5 us
  starting transfers between devices: 13 us -> 12.5 us
    ppermute x7 -> x3, starting transfers between devices: 8.34 us -> 4.45 us  [local(): part = lax.ppermute(part, 'screen', pairs)]
    ppermute x3 -> x7, starting transfers between devices: 4.65 us -> 8.03 us  [exchange(): return lax.ppermute(piece, ('depth', 'screen'), pairs)]
    ppermute x7 -> x3, waiting for transfers between devices: 3.11 us -> 5.1 us  [local(): part = lax.ppermute(part, 'screen', pairs)]
    ppermute x3 -> x7, waiting for transfers between devices: 5.58 us -> 6.4 us  [exchange(): return lax.ppermute(piece, ('depth', 'screen'), pairs)]
  transfers between devices with their start and end apart: 10 -> 10, of which waited for: 4 -> 4; matrix products, arithmetic and copies ran while one was open for 2% -> 2% of each run, Pallas kernels for 16% -> 15%
where the time goes in v3:
time: 36.5 us; the launch traced here: 36.2 us
  starting transfers between devices  12.5 us (34%)
  Pallas kernels  11.5 us (32%)
  waiting for transfers between devices  11.5 us (32%)
  local copies, waits for them, and re-layouts  0.71 us (2%)
    pallas_call x3, Pallas kernels, render(): pl.pallas_call(functools.partial(render_kernel, steps=steps, rate=rate),...  9.86 us
    ppermute x7, starting transfers between devices, exchange(): return lax.ppermute(piece, ('depth', 'screen'), pairs)  8.03 us
    ppermute x7, waiting for transfers between devices, exchange(): return lax.ppermute(piece, ('depth', 'screen'), pairs)  6.4 us
    ppermute x3, waiting for transfers between devices, local(): part = lax.ppermute(part, 'screen', pairs)  5.1 us
    ppermute x3, starting transfers between devices, local(): part = lax.ppermute(part, 'screen', pairs)  4.45 us
    pallas_call x1, Pallas kernels, composite(): pl.pallas_call(composite_kernel, out_shape=pltpu.VMEM((pair_count, channe...  0.91 us
  transfers between devices with their start and end apart: 10, of which 4 were waited for; matrix products, arithmetic and copies ran while one was open for 2% of the time, Pallas kernels for 15%

profile of v3, /device:TPU:0, one launch (start us, length us, event | category | flops | bytes accessed | tf_op | source)
XLA Modules:
  0.0 36.2 jit_solution(1280180999694384692)
XLA Ops:
  0.0 4.4 %render.4 = (f32[4,4,8,256]{3,2,1,0:T(8,128)S(1)}, f32[4,4,8,256]{3,2,1,0:T(8,128)S(1)}, f32[4,4,8,256]{3,2,1,0:T(8,128)S(1)}, f32[4,4,8,256]{3,2,1,0:T(8,128)S(1)}) custom-call(bf16[3,256]{1,0:T(4,128)(2,1)} %colors_hbm.5, bf16[256]{0:T(256)(128)(2,1)} %opacity_hbm.5, s32[8,256,256]{2,1,0:T(8,128)} %bins_hbm.5), custom_call_target="tpu_custom_call" | custom-call | tf_op jit(solution)/shard_map/render/pallas_call | solution.py:151
  4.4 3.0 %collective-permute-start = (f32[4,4,8,256]{3,2,1,0:T(8,128)S(1)}, f32[4,4,8,256]{3,2,1,0:T(8,128)S(1)}, u32[]{:S(2)}, u32[]{:S(2)}) collective-permute-start(f32[4,4,8,256]{3,2,1,0:T(8,128)S(1)} %get-tuple-element.14), channel_id=1, source_target_pairs={{0,8},{1,9},{2,10},{3,11},{4,12},{5,13},{6,14},{7,15},{8,0},{9,1},... | collective-permute-start | bytes 393224 | tf_op jit(solution)/shard_map/ppermute | solution.py:262
  7.4 0.0 copy-start
  7.4 1.5 %collective-permute-start.1 = (f32[4,4,8,256]{3,2,1,0:T(8,128)S(1)}, f32[4,4,8,256]{3,2,1,0:T(8,128)S(1)}, u32[]{:S(2)}, u32[]{:S(2)}) collective-permute-start(f32[4,4,8,256]{3,2,1,0:T(8,128)S(1)} %get-tuple-element.15), channel_id=1, source_target_pairs={{0,16},{1,17},{2,18},{3,19},{4,20},{5,21},{6,22},{7,23},{8,24},{9,... | collective-permute-start | bytes 393224 | tf_op jit(solution)/shard_map/ppermute | solution.py:262
  8.9 2.7 %render.5 = (f32[4,4,8,256]{3,2,1,0:T(8,128)S(1)}, f32[4,4,8,256]{3,2,1,0:T(8,128)S(1)}) custom-call(bf16[3,256]{1,0:T(4,128)(2,1)} %colors_hbm.5, bf16[256]{0:T(256)(128)(2,1)} %opacity_hbm.5, s32[8,256,256]{2,1,0:T(8,128)} %bins_hbm.5), custom_call_target="tpu_custom_call" | custom-call | tf_op jit(solution)/shard_map/render/pallas_call | solution.py:151
  11.7 0.1 collective-permute-start.2
  11.8 2.7 %render.3 = (f32[4,4,8,256]{3,2,1,0:T(8,128)S(1)}, f32[4,4,8,256]{3,2,1,0:T(8,128)S(1)}) custom-call(bf16[3,256]{1,0:T(4,128)(2,1)} %colors_hbm.5, bf16[256]{0:T(256)(128)(2,1)} %opacity_hbm.5, s32[8,256,256]{2,1,0:T(8,128)} %bins_hbm.5), custom_call_target="tpu_custom_call" | custom-call | tf_op jit(solution)/shard_map/render/pallas_call | solution.py:151
  14.5 0.1 collective-permute-start.3
  14.6 2.0 %collective-permute-start.4 = (f32[4,4,8,256]{3,2,1,0:T(8,128)S(1)}, f32[4,4,8,256]{3,2,1,0:T(8,128)S(1)}, u32[]{:S(2)}, u32[]{:S(2)}) collective-permute-start(f32[4,4,8,256]{3,2,1,0:T(8,128)S(1)} %get-tuple-element.18), channel_id=1, source_target_pairs={{0,9},{1,8},{2,11},{3,10},{4,13},{5,12},{6,15},{7,14},{8,1},{9,0},... | collective-permute-start | bytes 393224 | tf_op jit(solution)/shard_map/ppermute | solution.py:262
  16.7 0.0 collective-permute-done.refs_1_
  16.7 1.2 %collective-permute-start.5 = (f32[4,4,8,256]{3,2,1,0:T(8,128)S(1)}, f32[4,4,8,256]{3,2,1,0:T(8,128)S(1)}, u32[]{:S(2)}, u32[]{:S(2)}) collective-permute-start(f32[4,4,8,256]{3,2,1,0:T(8,128)S(1)} %get-tuple-element.19), channel_id=1, source_target_pairs={{0,17},{1,16},{2,19},{3,18},{4,21},{5,20},{6,23},{7,22},{8,25},{9,... | collective-permute-start | bytes 393224 | tf_op jit(solution)/shard_map/ppermute | solution.py:262
  17.9 0.0 collective-permute-done.1.refs_2_
  17.9 0.1 collective-permute-start.6
  17.9 0.0 copy-done
  17.9 0.7 %copy.5.order_ref = s32[8,4]{1,0:T(8,128)} copy(s32[8,4]{0,1:T(4,128)S(1)} %copy-done) | data formatting | bytes 256 | tf_op args[3]
  18.6 0.0 collective-permute-done.2.refs_3_
  18.6 0.0 collective-permute-done.3.refs_4_
  18.6 1.9 %collective-permute-done.4.refs_5_ = f32[4,4,8,256]{3,2,1,0:T(8,128)S(1)} collective-permute-done((f32[4,4,8,256]{3,2,1,0:T(8,128)S(1)}, f32[4,4,8,256]{3,2,1,0:T(8,128)S(1)}, u32[]{:S(2)}, u32[]{:S(2)}) %collective-permute-start.4) | collective-permute-done | bytes 131104 | tf_op jit(solution)/shard_map/ppermute | solution.py:262
  20.5 4.5 %collective-permute-done.5.refs_6_ = f32[4,4,8,256]{3,2,1,0:T(8,128)S(1)} collective-permute-done((f32[4,4,8,256]{3,2,1,0:T(8,128)S(1)}, f32[4,4,8,256]{3,2,1,0:T(8,128)S(1)}, u32[]{:S(2)}, u32[]{:S(2)}) %collective-permute-start.5) | collective-permute-done | bytes 131104 | tf_op jit(solution)/shard_map/ppermute | solution.py:262
  25.0 0.0 collective-permute-done.6.refs_7_
  25.0 0.9 %composite.1 = f32[4,4,8,512]{3,2,1,0:T(8,128)S(1)} custom-call(s32[8,4]{1,0:T(8,128)} %copy.5.order_ref, f32[4,4,8,256]{3,2,1,0:T(8,128)S(1)} %get-tuple-element.13.refs_0_, f32[4,4,8,256]{3,2,1,0:T(8,128)S(1)} %collective-permute-done.refs_1_, f32[4,4,8,256]{3,2,1,0:T(8,128)S(1)} %collective-permute-done.1.refs_2_, ...), custom_call_target="tpu_custom_call" | custom-call | tf_op jit(solution)/shard_map/composite/pallas_call | solution.py:206
  26.0 3.7 %collective-permute-start.7 = (f32[4,8,512]{2,1,0:T(8,128)S(1)}, f32[4,8,512]{2,1,0:T(8,128)S(1)}, u32[]{:S(2)}, u32[]{:S(2)}) collective-permute-start(f32[4,8,512]{2,1,0:T(8,128)S(1)} %get-tuple-element.24), channel_id=1, source_target_pairs={{0,6},{1,7},{2,4},{3,5},{4,2},{5,3},{6,0},{7,1},{8,14},{9,15},{10,... | collective-permute-start | bytes 196616 | tf_op jit(solution)/shard_map/ppermute | solution.py:281
  29.6 0.0 collective-permute-start.8
  29.6 0.8 %collective-permute-start.9 = (f32[4,8,512]{2,1,0:T(8,128)S(1)}, f32[4,8,512]{2,1,0:T(8,128)S(1)}, u32[]{:S(2)}, u32[]{:S(2)}) collective-permute-start(f32[4,8,512]{2,1,0:T(8,128)S(1)} %get-tuple-element.22), channel_id=1, source_target_pairs={{0,2},{1,3},{2,0},{3,1},{4,6},{5,7},{6,4},{7,5},{8,10},{9,11},{10,... | collective-permute-start | bytes 196616 | tf_op jit(solution)/shard_map/ppermute | solution.py:281
  30.4 1.8 %collective-permute-done.7.refs_0_ = f32[4,8,512]{2,1,0:T(8,128)S(1)} collective-permute-done((f32[4,8,512]{2,1,0:T(8,128)S(1)}, f32[4,8,512]{2,1,0:T(8,128)S(1)}, u32[]{:S(2)}, u32[]{:S(2)}) %collective-permute-start.7) | collective-permute-done | bytes 65568 | tf_op jit(solution)/shard_map/ppermute | solution.py:281
  32.2 3.3 %collective-permute-done.8.refs_1_ = f32[4,8,512]{2,1,0:T(8,128)S(1)} collective-permute-done((f32[4,8,512]{2,1,0:T(8,128)S(1)}, f32[4,8,512]{2,1,0:T(8,128)S(1)}, u32[]{:S(2)}, u32[]{:S(2)}) %collective-permute-start.8) | collective-permute-done | bytes 65568 | tf_op jit(solution)/shard_map/ppermute | solution.py:281
  35.5 0.0 collective-permute-done.9.refs_2_
  35.5 0.7 %assemble.1 = f32[4,8,2048]{2,1,0:T(8,128)} custom-call(f32[4,8,512]{2,1,0:T(8,128)S(1)} %collective-permute-done.7.refs_0_, f32[4,8,512]{2,1,0:T(8,128)S(1)} %collective-permute-done.8.refs_1_, f32[4,8,512]{2,1,0:T(8,128)S(1)} %collective-permute-done.9.refs_2_, f32[4,8,512]{2,1,0:T(8,128)S(1)} %get-tuple-element.21.refs_3_), custom_call_target="tpu_custom_call" | custom-call | tf_op jit(solution)/shard_map/assemble/pallas_call | solution.py:232
  (1 shorter events, 0.0 us)
Async XLA Ops:
  4.4 12.3 %collective-permute-start = (f32[4,4,8,256]{3,2,1,0:T(8,128)S(1)}, f32[4,4,8,256]{3,2,1,0:T(8,128)S(1)}, u32[]{:S(2)}, u32[]{:S(2)}) collective-permute-start(f32[4,4,8,256]{3,2,1,0:T(8,128)S(1)} %get-tuple-element.14), channel_id=1, source_target_pairs={{0,8},{1,9},{2,10},{3,11},{4,12},{5,13},{6,14},{7,15},{8,0},{9,1},... | collective-permute-start | bytes 393224 | tf_op jit(solution)/shard_map/ppermute | solution.py:262
  7.4 10.5 %copy-start = (s32[8,4]{0,1:T(4,128)S(1)}, s32[8,4]{0,1:T(4,128)}, u32[]{:S(2)}) copy-start(s32[8,4]{0,1:T(4,128)} %param.7) | copy-start | bytes 388
  7.4 10.4 %collective-permute-start.1 = (f32[4,4,8,256]{3,2,1,0:T(8,128)S(1)}, f32[4,4,8,256]{3,2,1,0:T(8,128)S(1)}, u32[]{:S(2)}, u32[]{:S(2)}) collective-permute-start(f32[4,4,8,256]{3,2,1,0:T(8,128)S(1)} %get-tuple-element.15), channel_id=1, source_target_pairs={{0,16},{1,17},{2,18},{3,19},{4,20},{5,21},{6,22},{7,23},{8,24},{9,... | collective-permute-start | bytes 393224 | tf_op jit(solution)/shard_map/ppermute | solution.py:262
  11.7 6.9 %collective-permute-start.2 = (f32[4,4,8,256]{3,2,1,0:T(8,128)S(1)}, f32[4,4,8,256]{3,2,1,0:T(8,128)S(1)}, u32[]{:S(2)}, u32[]{:S(2)}) collective-permute-start(f32[4,4,8,256]{3,2,1,0:T(8,128)S(1)} %get-tuple-element.16), channel_id=1, source_target_pairs={{0,24},{1,25},{2,26},{3,27},{4,28},{5,29},{6,30},{7,31},{8,16},{9,... | collective-permute-start | bytes 393224 | tf_op jit(solution)/shard_map/ppermute | solution.py:262
  14.5 4.1 %collective-permute-start.3 = (f32[4,4,8,256]{3,2,1,0:T(8,128)S(1)}, f32[4,4,8,256]{3,2,1,0:T(8,128)S(1)}, u32[]{:S(2)}, u32[]{:S(2)}) collective-permute-start(f32[4,4,8,256]{3,2,1,0:T(8,128)S(1)} %get-tuple-element.17), channel_id=1, source_target_pairs={{0,1},{1,0},{2,3},{3,2},{4,5},{5,4},{6,7},{7,6},{8,9},{9,8},{10,11... | collective-permute-start | bytes 393224 | tf_op jit(solution)/shard_map/ppermute | solution.py:262
  14.6 5.9 %collective-permute-start.4 = (f32[4,4,8,256]{3,2,1,0:T(8,128)S(1)}, f32[4,4,8,256]{3,2,1,0:T(8,128)S(1)}, u32[]{:S(2)}, u32[]{:S(2)}) collective-permute-start(f32[4,4,8,256]{3,2,1,0:T(8,128)S(1)} %get-tuple-element.18), channel_id=1, source_target_pairs={{0,9},{1,8},{2,11},{3,10},{4,13},{5,12},{6,15},{7,14},{8,1},{9,0},... | collective-permute-start | bytes 393224 | tf_op jit(solution)/shard_map/ppermute | solution.py:262
  16.7 8.3 %collective-permute-start.5 = (f32[4,4,8,256]{3,2,1,0:T(8,128)S(1)}, f32[4,4,8,256]{3,2,1,0:T(8,128)S(1)}, u32[]{:S(2)}, u32[]{:S(2)}) collective-permute-start(f32[4,4,8,256]{3,2,1,0:T(8,128)S(1)} %get-tuple-element.19), channel_id=1, source_target_pairs={{0,17},{1,16},{2,19},{3,18},{4,21},{5,20},{6,23},{7,22},{8,25},{9,... | collective-permute-start | bytes 393224 | tf_op jit(solution)/shard_map/ppermute | solution.py:262
  17.9 7.1 %collective-permute-start.6 = (f32[4,4,8,256]{3,2,1,0:T(8,128)S(1)}, f32[4,4,8,256]{3,2,1,0:T(8,128)S(1)}, u32[]{:S(2)}, u32[]{:S(2)}) collective-permute-start(f32[4,4,8,256]{3,2,1,0:T(8,128)S(1)} %get-tuple-element.20), channel_id=1, source_target_pairs={{0,25},{1,24},{2,27},{3,26},{4,29},{5,28},{6,31},{7,30},{8,17},{9,... | collective-permute-start | bytes 393224 | tf_op jit(solution)/shard_map/ppermute | solution.py:262
  26.0 6.3 %collective-permute-start.7 = (f32[4,8,512]{2,1,0:T(8,128)S(1)}, f32[4,8,512]{2,1,0:T(8,128)S(1)}, u32[]{:S(2)}, u32[]{:S(2)}) collective-permute-start(f32[4,8,512]{2,1,0:T(8,128)S(1)} %get-tuple-element.24), channel_id=1, source_target_pairs={{0,6},{1,7},{2,4},{3,5},{4,2},{5,3},{6,0},{7,1},{8,14},{9,15},{10,... | collective-permute-start | bytes 196616 | tf_op jit(solution)/shard_map/ppermute | solution.py:281
  29.6 5.9 %collective-permute-start.8 = (f32[4,8,512]{2,1,0:T(8,128)S(1)}, f32[4,8,512]{2,1,0:T(8,128)S(1)}, u32[]{:S(2)}, u32[]{:S(2)}) collective-permute-start(f32[4,8,512]{2,1,0:T(8,128)S(1)} %get-tuple-element.23), channel_id=1, source_target_pairs={{0,4},{1,5},{2,6},{3,7},{4,0},{5,1},{6,2},{7,3},{8,12},{9,13},{10,... | collective-permute-start | bytes 196616 | tf_op jit(solution)/shard_map/ppermute | solution.py:281
  29.6 5.9 %collective-permute-start.9 = (f32[4,8,512]{2,1,0:T(8,128)S(1)}, f32[4,8,512]{2,1,0:T(8,128)S(1)}, u32[]{:S(2)}, u32[]{:S(2)}) collective-permute-start(f32[4,8,512]{2,1,0:T(8,128)S(1)} %get-tuple-element.22), channel_id=1, source_target_pairs={{0,2},{1,3},{2,0},{3,1},{4,6},{5,7},{6,4},{7,5},{8,10},{9,11},{10,... | collective-permute-start | bytes 196616 | tf_op jit(solution)/shard_map/ppermute | solution.py:281
